TPU v7x, 32 devices: a whole 2x2x4 slice. The times are simulated.
32 devices in a mesh: tm: 8 (over y, x, core), sr: 4 (over z).
Axes of the slice: x: 2, y: 2, z: 4, core: 2. Of those that a mesh axis runs over, the one named last changes fastest.
Arguments:
- observations: bfloat16 [1024, 65536], P(None, ('sr', 'tm')), may hold values from -6 to 6
- loadings: float32 [65536, 128], P(('sr', 'tm')), may hold values from -0.0007324219 to 0.0007324219
- noise_precision: float32 [65536], P(('sr', 'tm')), may hold values from 0.5 to 4
- transition: float32 [128, 128], replicated, may hold values from -1 to 1, as said below
- filter_cov: float32 [128, 128], replicated, may hold values from -1 to 1, as said below
- smoother_gain: float32 [128, 128], replicated, may hold values from -1 to 1, as said below
- smoothed_cov: float32 [128, 128], replicated, may hold values from -1 to 1, as said below
Outputs:
- smoothed_factors: float32 [1024, 128], P('tm')
- new_loadings: float32 [65536, 128], P(('sr', 'tm'))
- new_transition: float32 [128, 128], replicated
Inputs may be any that keep to these rules, and one draw needn't show every extreme that they name: `transition`: the spectral radius is below one. `filter_cov`: symmetric positive definite. `smoother_gain`: the spectral radius is below one. `smoothed_cov`: symmetric positive definite.
All inputs are finite; a program needn't handle non-finite values.
Results may differ from a plain program's by a relative error of at most 0.00175.
The roundings to bfloat16 on the way count: a program that leaves them out, or rounds other values in their place, can miss the bound.
Values may be sent and summed in bfloat16 or wider, within the bound.
A program may use at most 64 MiB of HBM per device.

v0:
```python
import functools
import jax
import jax.numpy as jnp
from jax import lax
from jax.experimental import pallas as pl
from jax.experimental.pallas import tpu as pltpu
from jax.sharding import PartitionSpec as P

precise = lax.Precision.HIGHEST
MESH = pl.DeviceIdType.MESH
SLABS = 8
PIECES = 2
PIVOTS = 4


def dot_high(left, right):
    return jnp.dot(left, right, precision=precise, preferred_element_type=jnp.float32)


def dot_first(left, right):
    return lax.dot_general(
        left, right, (((0,), (0,)), ((), ())), precision=precise, preferred_element_type=jnp.float32
    )


def halves(value):
    high = value.astype(jnp.bfloat16)
    low = (value - high.astype(jnp.float32)).astype(jnp.bfloat16)
    return high, low


def weights(matrix):
    high, low = halves(matrix)
    side = jnp.concatenate([high, low], axis=1)
    return jnp.concatenate([side, side], axis=0)


def times(value, doubled):
    high, low = halves(value)
    width = value.shape[1]
    out = jnp.dot(
        jnp.concatenate([high, low], axis=1), doubled, preferred_element_type=jnp.float32
    )
    return out[:, :width] + out[:, width:]


def project_kernel(observations, loadings, precision, out):
    _, chips, rows, width = out.shape
    block = observations.shape[0] // (2 * chips)
    depth = loadings.shape[0]
    columns = [
        jnp.broadcast_to(precision[pl.ds(at, 1), :], (width, width)).T
        for at in range(depth // width)
    ]
    weighted = loadings[...] * jnp.concatenate(columns, axis=0)
    proj = jnp.dot(
        observations[...], weighted.astype(jnp.bfloat16), preferred_element_type=jnp.float32
    )
    left = jnp.concatenate(halves(loadings[...]), axis=1)
    right = jnp.concatenate(halves(weighted), axis=1)
    both = lax.dot_general(
        left, right, (((0,), (0,)), ((), ())), preferred_element_type=jnp.float32
    )
    both = both[:width] + both[width:]
    info = both[:, :width] + both[:, width:]
    share = width // (2 * chips)

    @pl.when(pl.program_id(0) == 0)
    def _():
        out[...] = jnp.zeros_like(out)

    for chip in range(chips):
        for core in range(2):
            at = 2 * chip + core
            out[core, chip, :block, :] += proj[at * block : (at + 1) * block]
            out[core, chip, block:, :] += info[at * share : (at + 1) * share]


def project(observations, loadings, noise_precision, blocks):
    length, series = observations.shape
    width = loadings.shape[1]
    depth = min(series, 512)
    lanes = depth // width
    shape = (2, blocks // 2, (length + width) // blocks, width)
    return pl.pallas_call(
        project_kernel,
        grid=(series // depth,),
        out_shape=jax.ShapeDtypeStruct(shape, jnp.float32),
        in_specs=[
            pl.BlockSpec((length, depth), lambda at: (0, at)),
            pl.BlockSpec((depth, width), lambda at: (at, 0)),
            pl.BlockSpec((None, lanes, width), lambda at: (at, 0, 0)),
        ],
        out_specs=pl.BlockSpec(shape, lambda at: (0, 0, 0, 0)),
        name="project",
    )(observations, loadings, noise_precision.reshape(series // depth, lanes, width))


def reduce_kernel(
    chips, planes, pieces, part, out, pair_in, mine, chip_in, plane_in,
    pair_send, pair_recv, chip_send, chip_recv, plane_send, plane_recv,
    back_send, back_recv, last_send, last_recv,
):
    tm = lax.axis_index("tm")
    sr = lax.axis_index("sr")
    core = lax.rem(tm, 2)
    chip = tm // 2
    other = 1 - core
    partner = (2 * chip + other, sr)

    def chip_at(step):
        return lax.rem(chip + step, chips)

    def plane_at(step):
        return lax.rem(sr + step, planes)

    barrier = pltpu.get_barrier_semaphore()
    pl.semaphore_signal(barrier, inc=1, device_id=partner, device_id_type=MESH)
    for step in range(1, chips):
        pl.semaphore_signal(
            barrier, inc=1, device_id=(2 * chip_at(step) + core, sr), device_id_type=MESH
        )
    for step in range(1, planes):
        pl.semaphore_signal(barrier, inc=1, device_id=(tm, plane_at(step)), device_id_type=MESH)
    pl.semaphore_wait(barrier, 1 + chips - 1 + planes - 1)

    order = list(range(1, chips)) + [0]
    pairs, across, along, back, last = {}, {}, {}, {}, {}
    for at, rows in enumerate(pieces):
        for step in order:
            target = chip_at(step)
            pairs[at, step] = pltpu.make_async_remote_copy(
                src_ref=part.at[other, target, rows],
                dst_ref=pair_in.at[step, rows],
                send_sem=pair_send.at[at, step],
                recv_sem=pair_recv.at[at, step],
                device_id=partner,
                device_id_type=MESH,
            )
            pairs[at, step].start()
    for at, rows in enumerate(pieces):
        for step in order:
            pairs[at, step].wait_recv()
            mine[step, rows] = part[core, chip_at(step), rows] + pair_in[step, rows]
            if step > 0:
                across[at, step] = pltpu.make_async_remote_copy(
                    src_ref=mine.at[step, rows],
                    dst_ref=chip_in.at[step, rows],
                    send_sem=chip_send.at[at, step],
                    recv_sem=chip_recv.at[at, step],
                    device_id=(2 * chip_at(step) + core, sr),
                    device_id_type=MESH,
                )
                across[at, step].start()
    for at, rows in enumerate(pieces):
        total = mine[0, rows]
        for step in range(1, chips):
            across[at, step].wait_recv()
            total = total + chip_in[step, rows]
        plane_in[sr, rows] = total
        for step in range(1, planes):
            along[at, step] = pltpu.make_async_remote_copy(
                src_ref=plane_in.at[sr, rows],
                dst_ref=plane_in.at[sr, rows],
                send_sem=plane_send.at[at, step],
                recv_sem=plane_recv.at[at, step],
                device_id=(tm, plane_at(step)),
                device_id_type=MESH,
            )
            along[at, step].start()

    def pass_on(at, rows, step):
        source = lax.rem(chip - step + chips, chips)
        last[at, step] = pltpu.make_async_remote_copy(
            src_ref=out.at[core, source, rows],
            dst_ref=out.at[core, source, rows],
            send_sem=last_send.at[at, step],
            recv_sem=last_recv.at[at, step],
            device_id=partner,
            device_id_type=MESH,
        )
        last[at, step].start()

    for at, rows in enumerate(pieces):
        for step in range(1, planes):
            along[at, step].wait_recv()
        whole = plane_in[0, rows]
        for plane in range(1, planes):
            whole = whole + plane_in[plane, rows]
        out[core, chip, rows] = whole
        for step in range(1, chips):
            back[at, step] = pltpu.make_async_remote_copy(
                src_ref=out.at[core, chip, rows],
                dst_ref=out.at[core, chip, rows],
                send_sem=back_send.at[at, step],
                recv_sem=back_recv.at[at, step],
                device_id=(2 * chip_at(step) + core, sr),
                device_id_type=MESH,
            )
            back[at, step].start()
        pass_on(at, rows, 0)
    for at, rows in enumerate(pieces):
        for step in range(1, chips):
            back[at, step].wait_recv()
            pass_on(at, rows, step)
    for copy in last.values():
        copy.wait_recv()
    for copies in (pairs, across, along, back, last):
        for copy in copies.values():
            copy.wait_send()


def all_sum(part, planes):
    _, chips, rows, width = part.shape
    dma = pltpu.SemaphoreType.DMA
    cuts = [rows * at // PIECES // 8 * 8 for at in range(PIECES)] + [rows]
    pieces = [slice(start, stop) for start, stop in zip(cuts, cuts[1:])]
    vmem = pl.BlockSpec(memory_space=pltpu.VMEM)
    return pl.pallas_call(
        functools.partial(reduce_kernel, chips, planes, pieces),
        out_shape=jax.ShapeDtypeStruct(part.shape, jnp.float32),
        in_specs=[vmem],
        out_specs=vmem,
        scratch_shapes=[
            pltpu.VMEM((chips, rows, width), jnp.float32),
            pltpu.VMEM((chips, rows, width), jnp.float32),
            pltpu.VMEM((chips, rows, width), jnp.float32),
            pltpu.VMEM((planes, rows, width), jnp.float32),
        ]
        + [dma((PIECES, chips))] * 4
        + [dma((PIECES, planes))] * 2
        + [dma((PIECES, chips))] * 4,
        compiler_params=pltpu.CompilerParams(collective_id=0, has_side_effects=True),
        name="all_sum",
    )(part)


def shift_rows(value, steps):
    length = value.shape[0]
    row = lax.broadcasted_iota(jnp.int32, value.shape, 0)
    moved = pltpu.roll(value, steps % length, 0)
    keep = row >= steps if steps > 0 else row < length + steps
    return jnp.where(keep, moved, 0.0)


def powers(matrix, count):
    low = [matrix]
    while len(low) < SLABS:
        low = low + [dot_high(low[-1], each) for each in low]
    high = []
    square = low[-1]
    for _ in range(count - 1):
        square = dot_high(square, square)
        high.append(square)
    return [weights(each) for each in low], [weights(low[-1])] + [weights(each) for each in high]


def scan_slabs(slabs, low, high, reverse):
    order = list(range(SLABS))[::-1] if reverse else list(range(SLABS))
    sign = -1 if reverse else 1
    part = {order[0]: slabs[order[0]]}
    for before, now in zip(order, order[1:]):
        part[now] = slabs[now] + times(part[before], low[0])
    ends = part[order[-1]]
    for level, power in enumerate(high):
        ends = ends + times(shift_rows(ends, sign * 2**level), power)
    carry = shift_rows(ends, sign)
    out = [None] * SLABS
    for place, now in enumerate(order[:-1]):
        out[now] = part[now] + times(carry, low[place])
    out[order[-1]] = ends
    return out


def inverse_two(a, b, c):
    scale = 1.0 / (a * c - b * b)
    return c * scale, -b * scale, a * scale


def inverse_four(p):
    e, f, g = inverse_two(p[0][0], p[0][1], p[1][1])
    u00 = e * p[0][2] + f * p[1][2]
    u01 = e * p[0][3] + f * p[1][3]
    u10 = f * p[0][2] + g * p[1][2]
    u11 = f * p[0][3] + g * p[1][3]
    s00 = p[2][2] - (p[0][2] * u00 + p[1][2] * u10)
    s01 = p[2][3] - (p[0][2] * u01 + p[1][2] * u11)
    s11 = p[3][3] - (p[0][3] * u01 + p[1][3] * u11)
    t00, t01, t11 = inverse_two(s00, s01, s11)
    v00 = u00 * t00 + u01 * t01
    v01 = u00 * t01 + u01 * t11
    v10 = u10 * t00 + u11 * t01
    v11 = u10 * t01 + u11 * t11
    a00 = e + (v00 * u00 + v01 * u01)
    a01 = f + (v00 * u10 + v01 * u11)
    a11 = g + (v10 * u10 + v11 * u11)
    return [
        [a00, a01, -v00, -v01],
        [a01, a11, -v10, -v11],
        [-v00, -v10, t00, t01],
        [-v01, -v11, t01, t11],
    ]


def invert(matrices):
    size = matrices[0].shape[0]
    row_at = lax.broadcasted_iota(jnp.int32, (size, size), 0)
    lane_at = lax.broadcasted_iota(jnp.int32, (size, size), 1)
    lane = lax.broadcasted_iota(jnp.int32, (8, size), 1)
    diagonal = row_at == lane_at
    scales, scaled = [], []
    for m in matrices:
        only = jnp.where(diagonal, m, 0.0)
        across = lax.rsqrt(jnp.sum(only, axis=0, keepdims=True))
        down = lax.rsqrt(jnp.sum(only, axis=1, keepdims=True))
        scales.append((across, down))
        scaled.append((m * across) * down)
    matrices = scaled
    for k in range(0, size, PIVOTS):
        following = []
        group = k // 8 * 8
        for m in matrices:
            columns = [jnp.broadcast_to(m[:, k + j : k + j + 1], m.shape) for j in range(PIVOTS)]

            def spread(value, at):
                return jnp.broadcast_to(value[at : at + 1, :], (8, size))

            block = [
                [spread(columns[j], k + min(i, j)) if i <= j else None for j in range(PIVOTS)]
                for i in range(PIVOTS)
            ]
            rows = [spread(m, k + i) for i in range(PIVOTS)]
            solved = inverse_four(block)
            fresh = []
            for i in range(PIVOTS):
                row = solved[i][0] * rows[0]
                for j in range(1, PIVOTS):
                    row = row + solved[i][j] * rows[j]
                for j in range(PIVOTS):
                    row = jnp.where(lane == k + j, solved[i][j], row)
                fresh.append(row)
            parts = []
            for start in range(0, size, 8):
                here = slice(start, start + 8)
                value = jnp.where((lane >= k) & (lane < k + PIVOTS), 0.0, m[here])
                take = columns[0][here] * fresh[0]
                for i in range(1, PIVOTS):
                    take = take + columns[i][here] * fresh[i]
                value = value - take
                if start == group:
                    for i in range(PIVOTS):
                        value = jnp.where(row_at[here] == k + i, fresh[i], value)
                parts.append(value)
            following.append(jnp.concatenate(parts, axis=0))
        matrices = following
    return [(m * across) * down for m, (across, down) in zip(matrices, scales)]


def smooth_kernel(
    total_in, transition, filter_cov, gain, cov, observations, own, updated, moved,
    drive, held, arrived,
):
    length = observations.shape[0]
    panel = pltpu.make_async_copy(observations, held, arrived)
    panel.start()
    width = transition.shape[0]
    _, chips, rows, _ = total_in.shape
    block = length // (2 * chips)
    count = length // SLABS
    levels = (count - 1).bit_length()
    info = jnp.concatenate(
        [total_in[core, chip, block:, :] for chip in range(chips) for core in range(2)], axis=0
    )
    closed = transition[...] - dot_high(filter_cov[...], dot_high(info, transition[...]))
    low, high = powers(closed.T, levels)
    cov_t = weights(filter_cov[...].T)
    for chip in range(chips):
        for core in range(2):
            start = (2 * chip + core) * block
            drive[start : start + block, :] = times(total_in[core, chip, :block, :], cov_t)
    slabs = [drive[pl.ds(at, count, stride=SLABS), :] for at in range(SLABS)]
    filtered = scan_slabs(slabs, low, high, False)
    coupled = weights(dot_high(gain[...], transition[...]).T)
    last = lax.broadcasted_iota(jnp.int32, (count, width), 0) == count - 1
    back = [each - times(each, coupled) for each in filtered]
    back[-1] = jnp.where(last, filtered[-1], back[-1])
    low, high = powers(gain[...].T, levels)
    smooth = scan_slabs(back, low, high, True)
    for at in range(SLABS):
        drive[pl.ds(at, count, stride=SLABS), :] = smooth[at]
    place = pl.multiple_of(lax.axis_index("tm") * block, block)
    own[...] = drive[pl.ds(place, block), :]
    kept = smooth[:-1] + [jnp.where(last, 0.0, smooth[-1])]
    previous = sum(dot_first(each, each) for each in kept)
    final = smooth[-1][count - 8 :, :]
    final = jnp.where(lax.broadcasted_iota(jnp.int32, final.shape, 0) == 7, final, 0.0)
    total = previous + dot_first(final, final)
    lag = [shift_rows(smooth[-1], 1)] + smooth[:-1]
    lagged = sum(dot_first(each, before) for each, before in zip(smooth, lag))
    total = total + length * cov[...]
    previous = previous + (length - 1) * cov[...]
    lagged = lagged + (length - 1) * dot_high(cov[...], gain[...].T)
    factors = drive[...].T.astype(jnp.bfloat16)
    panel.wait()
    series = updated.shape[0]
    parts = [slice(start, min(start + 256, series)) for start in range(0, series, 256)]
    for part in parts:
        updated[part, :] = jnp.dot(
            factors, held[:, part], preferred_element_type=jnp.float32
        ).T
    total, previous = invert([total, previous])
    total = weights(total)
    for part in parts:
        updated[part, :] = times(updated[part, :], total)
    moved[...] = dot_high(lagged, previous)


def local(
    observations, loadings, noise_precision, transition, filter_cov, smoother_gain, smoothed_cov
):
    blocks = lax.axis_size("tm")
    planes = lax.axis_size("sr")
    width = transition.shape[0]
    length = observations.shape[0]
    steps_dev = length // blocks
    part = project(observations, loadings, noise_precision, blocks)
    summed = all_sum(part, planes)
    vmem = pl.BlockSpec(memory_space=pltpu.VMEM)
    series = observations.shape[1]
    return pl.pallas_call(
        smooth_kernel,
        out_shape=[
            jax.ShapeDtypeStruct((steps_dev, width), jnp.float32),
            jax.ShapeDtypeStruct((series, width), jnp.float32),
            jax.ShapeDtypeStruct((width, width), jnp.float32),
        ],
        in_specs=[vmem] * 5 + [pl.BlockSpec(memory_space=pl.ANY)],
        out_specs=[vmem] * 3,
        scratch_shapes=[
            pltpu.VMEM((length, width), jnp.float32),
            pltpu.VMEM((length, series), observations.dtype),
            pltpu.SemaphoreType.DMA,
        ],
        name="smooth",
    )(summed, transition, filter_cov, smoother_gain, smoothed_cov, observations)


def solution(mesh):
    in_specs = (P(None, ("sr", "tm")), P(("sr", "tm"), None), P(("sr", "tm")), P(), P(), P(), P())
    out_specs = (P("tm", None), P(("sr", "tm"), None), P())
    return jax.shard_map(local, mesh=mesh, in_specs=in_specs, out_specs=out_specs, check_vma=False)
```

profile of v0, /device:TPU:0, one launch (start us, length us, event | category | flops | bytes accessed | tf_op | source)
XLA Modules:
  0.0 53.2 jit_solution(6535441535178301660)
XLA Ops:
  0.6 5.6 %project.1.part = f32[2,4,144,128]{3,2,1,0:T(8,128)} custom-call(bf16[1024,2048]{1,0:T(8,128)(2,1)} %observations.3, f32[2048,128]{1,0:T(8,128)} %loadings.1, f32[4,4,128]{2,1,0:T(4,128)} %bitcast.1), custom_call_target="tpu_custom_call" | custom-call | tf_op jit(solution)/shard_map/project/pallas_call | solution.py:85
  6.2 25.1 %all_sum.1.total_in = f32[2,4,144,128]{3,2,1,0:T(8,128)} custom-call(f32[2,4,144,128]{3,2,1,0:T(8,128)} %project.1.part), custom_call_target="tpu_custom_call" | custom-call | tf_op jit(solution)/shard_map/all_sum/pallas_call | solution.py:219
  31.3 21.8 %smooth.1 = (f32[128,128]{1,0:T(8,128)}, f32[2048,128]{1,0:T(8,128)}, f32[128,128]{1,0:T(8,128)}) custom-call(f32[2,4,144,128]{3,2,1,0:T(8,128)} %all_sum.1.total_in, f32[128,128]{1,0:T(8,128)} %transition.1, f32[128,128]{1,0:T(8,128)} %filter_cov.1, f32[128,128]{1,0:T(8,128)} %gain.1, f32[128,128]{1,0:T(8,128)} %cov.1, bf16[1024,2048]{1,0:T(8,128)(2,1)} %observations.3), custom_call_target="tpu_custom_call" | custom-call | tf_op jit(solution)/shard_map/smooth/pallas_call | solution.py:430
where the time goes:
time: 53.5 us; the launch traced here: 53.2 us
  Pallas kernels  52.4 us (98%)
  between operations  0.8 us (1%)
    pallas_call x1, Pallas kernels, all_sum(): pl.pallas_call(functools.partial(reduce_kernel, chips, planes, pieces), o...  25.1 us
    pallas_call x1, Pallas kernels, local(): pl.pallas_call(smooth_kernel, out_shape=[jax.ShapeDtypeStruct((steps_dev,...  21.8 us
    pallas_call x1, Pallas kernels, project(): pl.pallas_call(project_kernel, grid=(series // depth,), out_shape=jax.Sha...  5.55 us

commit v1 on v0

--- a/solution.py
+++ b/solution.py
@@ -302,11 +302,73 @@
     ]
 
 
+def dot_last(left, right):
+    return lax.dot_general(left, right, (((1,), (1,)), ((), ())), precision=precise, preferred_element_type=jnp.float32)
+
+
+def pick(value, lane, half, at):
+    index = jnp.where(lane >= half, half + at, at)
+    return jnp.take_along_axis(value, index, axis=1, mode="promise_in_bounds")
+
+def sweep(packed):
+    half, size = packed.shape
+    lane = lax.broadcasted_iota(jnp.int32, (8, size), 1)
+    inner = jnp.where(lane >= half, lane - half, lane)
+    sub = lax.broadcasted_iota(jnp.int32, (8, size), 0)
+    groups = half // 8
+    value = [packed[8 * g : 8 * g + 8] for g in range(groups)]
+
+    def spread(tile, at):
+        return jnp.broadcast_to(tile[at : at + 1, :], (8, size))
+
+    first = [pick(value[0], lane, half, j) for j in range(PIVOTS)]
+    block = [[spread(first[max(i, j)], min(i, j)) for j in range(PIVOTS)] for i in range(PIVOTS)]
+    for k in range(0, half, PIVOTS):
+        group, place = divmod(k, 8)
+        solved = inverse_four(block)
+        order = list(range(groups))
+        following = k + PIVOTS
+        if following < half:
+            ahead, spot = divmod(following, 8)
+            order.remove(ahead)
+            order.insert(0, ahead)
+        columns = [None] * groups
+        for g in order:
+            columns[g] = [pick(value[g], lane, half, k + j) for j in range(PIVOTS)]
+            if g == order[0] and following < half:
+                coming = [pick(value[g], lane, half, following + j) for j in range(PIVOTS)]
+        if following < half:
+            cross = [[spread(columns[ahead][j], spot + i) for j in range(PIVOTS)] for i in range(PIVOTS)]
+            moved = [[sum(solved[i][j] * cross[b][j] for j in range(PIVOTS)) for b in range(PIVOTS)] for i in range(PIVOTS)]
+            block = [[None] * PIVOTS for _ in range(PIVOTS)]
+            for a in range(PIVOTS):
+                for b in range(a, PIVOTS):
+                    take = sum(cross[a][i] * moved[i][b] for i in range(PIVOTS))
+                    block[a][b] = block[b][a] = spread(coming[b], spot + a) - take
+        here = (inner >= k) & (inner < k + PIVOTS)
+        rows = []
+        for i in range(PIVOTS):
+            row = jnp.where(here, 0.0, spread(value[group], place + i))
+            rows.append(jnp.where(inner == k + i, 1.0, row))
+        fresh = [sum(solved[i][j] * rows[j] for j in range(PIVOTS)) for i in range(PIVOTS)]
+        updated = [None] * groups
+        for g in order:
+            take = sum(columns[g][i] * fresh[i] for i in range(PIVOTS))
+            updated[g] = jnp.where(here, 0.0, value[g]) - take
+            if g == group:
+                for i in range(PIVOTS):
+                    updated[g] = jnp.where(sub == place + i, fresh[i], updated[g])
+        value = updated
+    return jnp.concatenate(value, axis=0)
+
+
 def invert(matrices):
     size = matrices[0].shape[0]
+    half = size // 2
     row_at = lax.broadcasted_iota(jnp.int32, (size, size), 0)
     lane_at = lax.broadcasted_iota(jnp.int32, (size, size), 1)
-    lane = lax.broadcasted_iota(jnp.int32, (8, size), 1)
+    low = lax.broadcasted_iota(jnp.int32, (half, size), 1) < half
+    nothing = jnp.zeros((half, size), jnp.float32)
     diagonal = row_at == lane_at
     scales, scaled = [], []
     for m in matrices:
@@ -315,45 +377,24 @@
         down = lax.rsqrt(jnp.sum(only, axis=1, keepdims=True))
         scales.append((across, down))
         scaled.append((m * across) * down)
-    matrices = scaled
-    for k in range(0, size, PIVOTS):
-        following = []
-        group = k // 8 * 8
-        for m in matrices:
-            columns = [jnp.broadcast_to(m[:, k + j : k + j + 1], m.shape) for j in range(PIVOTS)]
-
-            def spread(value, at):
-                return jnp.broadcast_to(value[at : at + 1, :], (8, size))
-
-            block = [
-                [spread(columns[j], k + min(i, j)) if i <= j else None for j in range(PIVOTS)]
-                for i in range(PIVOTS)
-            ]
-            rows = [spread(m, k + i) for i in range(PIVOTS)]
-            solved = inverse_four(block)
-            fresh = []
-            for i in range(PIVOTS):
-                row = solved[i][0] * rows[0]
-                for j in range(1, PIVOTS):
-                    row = row + solved[i][j] * rows[j]
-                for j in range(PIVOTS):
-                    row = jnp.where(lane == k + j, solved[i][j], row)
-                fresh.append(row)
-            parts = []
-            for start in range(0, size, 8):
-                here = slice(start, start + 8)
-                value = jnp.where((lane >= k) & (lane < k + PIVOTS), 0.0, m[here])
-                take = columns[0][here] * fresh[0]
-                for i in range(1, PIVOTS):
-                    take = take + columns[i][here] * fresh[i]
-                value = value - take
-                if start == group:
-                    for i in range(PIVOTS):
-                        value = jnp.where(row_at[here] == k + i, fresh[i], value)
-                parts.append(value)
-            following.append(jnp.concatenate(parts, axis=0))
-        matrices = following
-    return [(m * across) * down for m, (across, down) in zip(matrices, scales)]
+    one, two = scaled
+    packed = sweep(jnp.where(low, one[:half], pltpu.roll(two[:half], half, 1)))
+    corner = [jnp.where(low, packed, 0.0), jnp.where(low, pltpu.roll(packed, half, 1), 0.0)]
+    upper, rest = [], []
+    for m, each in zip(scaled, corner):
+        over = jnp.where(low, 0.0, dot_high(each, m))
+        over = jnp.concatenate([over, nothing], axis=0)
+        upper.append(over)
+        rest.append(m[half:] - dot_high(jnp.where(low, m[half:], 0.0), over))
+    packed = sweep(jnp.where(low, pltpu.roll(rest[1], half, 1), rest[0]))
+    final = [jnp.where(low, 0.0, packed), jnp.where(low, 0.0, pltpu.roll(packed, half, 1))]
+    out = []
+    for each, over, last, (across, down) in zip(corner, upper, final, scales):
+        side = dot_high(over[:half], jnp.concatenate([nothing, last], axis=0))
+        top = each + dot_last(side, over) - side
+        bottom = last - dot_last(last, over)
+        out.append((jnp.concatenate([top, bottom], axis=0) * across) * down)
+    return out
 
 
 def smooth_kernel(
@@ -390,17 +431,26 @@
         drive[pl.ds(at, count, stride=SLABS), :] = smooth[at]
     place = pl.multiple_of(lax.axis_index("tm") * block, block)
     own[...] = drive[pl.ds(place, block), :]
-    kept = smooth[:-1] + [jnp.where(last, 0.0, smooth[-1])]
-    previous = sum(dot_first(each, each) for each in kept)
+    whole = drive[...]
+    high, rest = halves(whole)
+    factors = high.T
+    time = lax.broadcasted_iota(jnp.int32, whole.shape, 0)
+    kept = halves(jnp.where(time == length - 1, 0.0, whole))
+    lag = halves(shift_rows(whole, 1))
+    sums = jnp.dot(
+        jnp.concatenate([factors, rest.T], axis=0),
+        jnp.concatenate(kept + lag, axis=1),
+        preferred_element_type=jnp.float32,
+    )
+    sums = sums[:width] + sums[width:]
+    previous = sums[:, :width] + sums[:, width : 2 * width]
+    lagged = sums[:, 2 * width : 3 * width] + sums[:, 3 * width :]
     final = smooth[-1][count - 8 :, :]
     final = jnp.where(lax.broadcasted_iota(jnp.int32, final.shape, 0) == 7, final, 0.0)
     total = previous + dot_first(final, final)
-    lag = [shift_rows(smooth[-1], 1)] + smooth[:-1]
-    lagged = sum(dot_first(each, before) for each, before in zip(smooth, lag))
     total = total + length * cov[...]
     previous = previous + (length - 1) * cov[...]
     lagged = lagged + (length - 1) * dot_high(cov[...], gain[...].T)
-    factors = drive[...].T.astype(jnp.bfloat16)
     panel.wait()
     series = updated.shape[0]
     parts = [slice(start, min(start + 256, series)) for start in range(0, series, 256)]

time: 53.5 us -> 48.4 us (0.905)
  Pallas kernels: 52.4 us -> 47.5 us
    pallas_call x1, Pallas kernels: 21.8 us -> 16.9 us  [local(): pl.pallas_call(smooth_kernel, out_shape=[jax.ShapeDtypeStruct((steps_dev,...]
where the time goes in v1:
time: 48.4 us; the launch traced here: 48.2 us
  Pallas kernels  47.5 us (98%)
  between operations  0.64 us (1%)
    pallas_call x1, Pallas kernels, all_sum(): pl.pallas_call(functools.partial(reduce_kernel, chips, planes, pieces), o...  25.1 us
    pallas_call x1, Pallas kernels, local(): pl.pallas_call(smooth_kernel, out_shape=[jax.ShapeDtypeStruct((steps_dev,...  16.9 us
    pallas_call x1, Pallas kernels, project(): pl.pallas_call(project_kernel, grid=(series // depth,), out_shape=jax.Sha...  5.55 us

profile of v1, /device:TPU:0, one launch (start us, length us, event | category | flops | bytes accessed | tf_op | source)
XLA Modules:
  0.0 48.2 jit_solution(12494860758762749551)
XLA Ops:
  0.6 5.5 %project.1.part = f32[2,4,144,128]{3,2,1,0:T(8,128)} custom-call(bf16[1024,2048]{1,0:T(8,128)(2,1)} %observations.3, f32[2048,128]{1,0:T(8,128)} %loadings.1, f32[4,4,128]{2,1,0:T(4,128)} %bitcast.1), custom_call_target="tpu_custom_call" | custom-call | tf_op jit(solution)/shard_map/project/pallas_call | solution.py:85
  6.2 25.1 %all_sum.1.total_in = f32[2,4,144,128]{3,2,1,0:T(8,128)} custom-call(f32[2,4,144,128]{3,2,1,0:T(8,128)} %project.1.part), custom_call_target="tpu_custom_call" | custom-call | tf_op jit(solution)/shard_map/all_sum/pallas_call | solution.py:219
  31.3 16.9 %smooth.1 = (f32[128,128]{1,0:T(8,128)}, f32[2048,128]{1,0:T(8,128)}, f32[128,128]{1,0:T(8,128)}) custom-call(f32[2,4,144,128]{3,2,1,0:T(8,128)} %all_sum.1.total_in, f32[128,128]{1,0:T(8,128)} %transition.1, f32[128,128]{1,0:T(8,128)} %filter_cov.1, f32[128,128]{1,0:T(8,128)} %gain.1, f32[128,128]{1,0:T(8,128)} %cov.1, bf16[1024,2048]{1,0:T(8,128)(2,1)} %observations.3), custom_call_target="tpu_custom_call" | custom-call | tf_op jit(solution)/shard_map/smooth/pallas_call | solution.py:480

commit v2 on v1

--- a/solution.py
+++ b/solution.py
@@ -9,7 +9,6 @@
 precise = lax.Precision.HIGHEST
 MESH = pl.DeviceIdType.MESH
 SLABS = 8
-PIECES = 2
 PIVOTS = 4
 
 
@@ -44,195 +43,241 @@
     return out[:, :width] + out[:, width:]
 
 
-def project_kernel(observations, loadings, precision, out):
-    _, chips, rows, width = out.shape
-    block = observations.shape[0] // (2 * chips)
-    depth = loadings.shape[0]
-    columns = [
-        jnp.broadcast_to(precision[pl.ds(at, 1), :], (width, width)).T
-        for at in range(depth // width)
-    ]
-    weighted = loadings[...] * jnp.concatenate(columns, axis=0)
-    proj = jnp.dot(
-        observations[...], weighted.astype(jnp.bfloat16), preferred_element_type=jnp.float32
-    )
-    left = jnp.concatenate(halves(loadings[...]), axis=1)
-    right = jnp.concatenate(halves(weighted), axis=1)
-    both = lax.dot_general(
-        left, right, (((0,), (0,)), ((), ())), preferred_element_type=jnp.float32
-    )
-    both = both[:width] + both[width:]
-    info = both[:, :width] + both[:, width:]
-    share = width // (2 * chips)
-
-    @pl.when(pl.program_id(0) == 0)
-    def _():
-        out[...] = jnp.zeros_like(out)
-
-    for chip in range(chips):
-        for core in range(2):
-            at = 2 * chip + core
-            out[core, chip, :block, :] += proj[at * block : (at + 1) * block]
-            out[core, chip, block:, :] += info[at * share : (at + 1) * share]
-
-
-def project(observations, loadings, noise_precision, blocks):
-    length, series = observations.shape
-    width = loadings.shape[1]
-    depth = min(series, 512)
-    lanes = depth // width
-    shape = (2, blocks // 2, (length + width) // blocks, width)
-    return pl.pallas_call(
-        project_kernel,
-        grid=(series // depth,),
-        out_shape=jax.ShapeDtypeStruct(shape, jnp.float32),
-        in_specs=[
-            pl.BlockSpec((length, depth), lambda at: (0, at)),
-            pl.BlockSpec((depth, width), lambda at: (at, 0)),
-            pl.BlockSpec((None, lanes, width), lambda at: (at, 0, 0)),
-        ],
-        out_specs=pl.BlockSpec(shape, lambda at: (0, 0, 0, 0)),
-        name="project",
-    )(observations, loadings, noise_precision.reshape(series // depth, lanes, width))
-
-
-def reduce_kernel(
-    chips, planes, pieces, part, out, pair_in, mine, chip_in, plane_in,
-    pair_send, pair_recv, chip_send, chip_recv, plane_send, plane_recv,
-    back_send, back_recv, last_send, last_recv,
+def gather_kernel(
+    blocks, planes, observations, loadings, precision, out, out_info,
+    panel, rows_in, part, part_info, *scratch,
 ):
+    chips = blocks // 2
+    _, _, lows, rows, width = part.shape
+    highs = planes // lows
+    length, series = panel.shape
+    share = part_info.shape[3]
+    block = length // blocks
+    steps = chips * lows
     tm = lax.axis_index("tm")
     sr = lax.axis_index("sr")
     core = lax.rem(tm, 2)
     chip = tm // 2
     other = 1 - core
+    low = lax.rem(sr, lows)
+    high = sr // lows
     partner = (2 * chip + other, sr)
+    order = list(range(lows, steps)) + list(range(lows))[::-1]
 
     def chip_at(step):
-        return lax.rem(chip + step, chips)
-
-    def plane_at(step):
-        return lax.rem(sr + step, planes)
+        return lax.rem(chip + step // lows, chips)
+
+    def low_at(step):
+        return lax.rem(low + step % lows, lows)
+
+    def member(step):
+        return (2 * chip_at(step) + core, high * lows + low_at(step))
+
+    def level(step):
+        return (tm, lax.rem(high + step, highs) * lows + low)
+
+    loads_done, panel_done = scratch[:2]
+    pieces = loads_done.shape[0]
+    depth = series // pieces
+    loads = []
+    for at in range(pieces):
+        here = slice(at * depth, (at + 1) * depth)
+        loads.append(
+            pltpu.make_async_copy(loadings.at[here, :], rows_in.at[here, :], loads_done.at[at])
+        )
+        loads[-1].start()
+    tall = 2 * block
+    panels = {}
+    for step in list(range(1, chips)) + [0]:
+        start = pl.multiple_of(lax.rem(chip + step, chips) * tall, tall)
+        panels[step] = pltpu.make_async_copy(
+            observations.at[pl.ds(start, tall), :],
+            panel.at[pl.ds(start, tall), :],
+            panel_done.at[step],
+        )
+        panels[step].start()
 
     barrier = pltpu.get_barrier_semaphore()
     pl.semaphore_signal(barrier, inc=1, device_id=partner, device_id_type=MESH)
-    for step in range(1, chips):
-        pl.semaphore_signal(
-            barrier, inc=1, device_id=(2 * chip_at(step) + core, sr), device_id_type=MESH
+    for step in range(1, steps):
+        pl.semaphore_signal(barrier, inc=1, device_id=member(step), device_id_type=MESH)
+    for step in range(1, highs):
+        pl.semaphore_signal(barrier, inc=1, device_id=level(step), device_id_type=MESH)
+
+    both = None
+    weighted = []
+    for at in range(pieces):
+        here = slice(at * depth, (at + 1) * depth)
+        columns = [
+            jnp.broadcast_to(precision[pl.ds(row, 1), :], (width, width)).T
+            for row in range(at * depth // width, (at + 1) * depth // width)
+        ]
+        loads[at].wait()
+        value = rows_in[here, :]
+        scaled = value * jnp.concatenate(columns, axis=0)
+        pair = halves(scaled)
+        weighted.append(pair[0])
+        left = jnp.concatenate(halves(value), axis=1)
+        right = jnp.concatenate(pair, axis=1)
+        each = lax.dot_general(
+            left, right, (((0,), (0,)), ((), ())), preferred_element_type=jnp.float32
         )
-    for step in range(1, planes):
-        pl.semaphore_signal(barrier, inc=1, device_id=(tm, plane_at(step)), device_id_type=MESH)
-    pl.semaphore_wait(barrier, 1 + chips - 1 + planes - 1)
-
-    order = list(range(1, chips)) + [0]
-    pairs, across, along, back, last = {}, {}, {}, {}, {}
-    for at, rows in enumerate(pieces):
+        both = each if both is None else both + each
+    weighted = jnp.concatenate(weighted, axis=0)
+    both = both[:width] + both[width:]
+    info = both[:, :width] + both[:, width:]
+    for place in range(2 * steps):
+        now = slice(place * share, (place + 1) * share)
+        part_info[place // lows % 2, place // (2 * lows), place % lows] = info[now]
+    pl.semaphore_wait(barrier, 1 + steps - 1 + highs - 1)
+
+    class Stream:
+        def __init__(self, part, out, pair_in, mine, cube_in, far_in, pair, across, far, back, last):
+            self.part, self.out = part, out
+            self.pair_in, self.mine, self.cube_in, self.far_in = pair_in, mine, cube_in, far_in
+            self.pair, self.across, self.far, self.back, self.last = pair, across, far, back, last
+            self.sent = []
+            self.open = {}
+
+        def send(self, key, source, target, semaphores, at, device):
+            copy = pltpu.make_async_remote_copy(
+                src_ref=source, dst_ref=target,
+                send_sem=semaphores.at[0, at], recv_sem=semaphores.at[1, at],
+                device_id=device, device_id_type=MESH,
+            )
+            copy.start()
+            self.open[key] = copy
+            self.sent.append(copy)
+
+        def wait(self, key):
+            self.open[key].wait_recv()
+
+        def to_pair(self, step):
+            source = self.part.at[other, chip_at(step), low_at(step)]
+            self.send(("pair", step), source, self.pair_in.at[step], self.pair, step, partner)
+
+        def to_cube(self, step):
+            self.wait(("pair", step))
+            self.mine[step] = self.part[core, chip_at(step), low_at(step)] + self.pair_in[step]
+            if step > 0:
+                self.send(
+                    ("across", step), self.mine.at[step], self.cube_in.at[step],
+                    self.across, step, member(step),
+                )
+
+        def to_far(self):
+            total = self.mine[0]
+            for step in order[:-1]:
+                self.wait(("across", step))
+                total = total + self.cube_in[step]
+            self.far_in[high] = total
+            for step in range(1, highs):
+                self.send(
+                    ("far", step), self.far_in.at[high], self.far_in.at[high],
+                    self.far, step, level(step),
+                )
+
+        def to_back(self):
+            for step in range(1, highs):
+                self.wait(("far", step))
+            total = self.far_in[0]
+            for step in range(1, highs):
+                total = total + self.far_in[step]
+            here = self.out.at[core, chip, low]
+            here[...] = total
+            for step in order[:-1]:
+                self.send(("back", step), here, here, self.back, step, member(step))
+            self.send(("last", 0), here, here, self.last, 0, partner)
+
+        def to_last(self, step):
+            self.wait(("back", step))
+            source = lax.rem(chip + chips - step // lows, chips)
+            here = self.out.at[core, source, lax.rem(low + lows - step % lows, lows)]
+            self.send(("last", step), here, here, self.last, step, partner)
+
+    small = Stream(part_info, out_info, *scratch[2:11])
+    large = Stream(part, out, *scratch[11:20])
+    for step in order:
+        small.to_pair(step)
+    waiting = []
+    for turn in list(range(1, chips)) + [0]:
+        panels[turn].wait()
+        source = lax.rem(chip + turn, chips)
+        start = pl.multiple_of(source * tall, tall)
+        proj = jnp.dot(
+            panel[pl.ds(start, tall), :], weighted, preferred_element_type=jnp.float32
+        )
+        for at in range(2):
+            for half in range(lows):
+                now = slice(at * block + half * rows, at * block + (half + 1) * rows)
+                part[at, source, half] = proj[now]
+        fresh = [step for step in order if step // lows == turn]
+        for step in fresh:
+            large.to_pair(step)
+        if turn == 1 % chips:
+            for step in order:
+                small.to_cube(step)
+        for step in waiting:
+            large.to_cube(step)
+        waiting = fresh
+    for step in waiting:
+        large.to_cube(step)
+    small.to_far()
+    large.to_far()
+    small.to_back()
+    large.to_back()
+    for stream in (small, large):
+        for step in order[:-1]:
+            stream.to_last(step)
+    for stream in (small, large):
         for step in order:
-            target = chip_at(step)
-            pairs[at, step] = pltpu.make_async_remote_copy(
-                src_ref=part.at[other, target, rows],
-                dst_ref=pair_in.at[step, rows],
-                send_sem=pair_send.at[at, step],
-                recv_sem=pair_recv.at[at, step],
-                device_id=partner,
-                device_id_type=MESH,
-            )
-            pairs[at, step].start()
-    for at, rows in enumerate(pieces):
-        for step in order:
-            pairs[at, step].wait_recv()
-            mine[step, rows] = part[core, chip_at(step), rows] + pair_in[step, rows]
-            if step > 0:
-                across[at, step] = pltpu.make_async_remote_copy(
-                    src_ref=mine.at[step, rows],
-                    dst_ref=chip_in.at[step, rows],
-                    send_sem=chip_send.at[at, step],
-                    recv_sem=chip_recv.at[at, step],
-                    device_id=(2 * chip_at(step) + core, sr),
-                    device_id_type=MESH,
-                )
-                across[at, step].start()
-    for at, rows in enumerate(pieces):
-        total = mine[0, rows]
-        for step in range(1, chips):
-            across[at, step].wait_recv()
-            total = total + chip_in[step, rows]
-        plane_in[sr, rows] = total
-        for step in range(1, planes):
-            along[at, step] = pltpu.make_async_remote_copy(
-                src_ref=plane_in.at[sr, rows],
-                dst_ref=plane_in.at[sr, rows],
-                send_sem=plane_send.at[at, step],
-                recv_sem=plane_recv.at[at, step],
-                device_id=(tm, plane_at(step)),
-                device_id_type=MESH,
-            )
-            along[at, step].start()
-
-    def pass_on(at, rows, step):
-        source = lax.rem(chip - step + chips, chips)
-        last[at, step] = pltpu.make_async_remote_copy(
-            src_ref=out.at[core, source, rows],
-            dst_ref=out.at[core, source, rows],
-            send_sem=last_send.at[at, step],
-            recv_sem=last_recv.at[at, step],
-            device_id=partner,
-            device_id_type=MESH,
+            stream.wait(("last", step))
+    for stream in (small, large):
+        for copy in stream.sent:
+            copy.wait_send()
+
+
+def gather(observations, loadings, noise_precision, blocks, planes):
+    length, series = observations.shape
+    width = loadings.shape[1]
+    chips = blocks // 2
+    lows = 2 if planes % 2 == 0 else 1
+    highs = planes // lows
+    rows = length // (blocks * lows)
+    share = width // (blocks * lows)
+    pieces = min(4, series // width)
+    dma = pltpu.SemaphoreType.DMA
+    vmem = pl.BlockSpec(memory_space=pltpu.VMEM)
+    hbm = pl.BlockSpec(memory_space=pl.ANY)
+    steps = chips * lows
+
+    def memory(*shape):
+        return pltpu.VMEM(shape, jnp.float32)
+
+    def stream(tall):
+        return [memory(steps, tall, width)] * 3 + [memory(highs, tall, width)] + (
+            [dma((2, steps))] * 2 + [dma((2, highs))] + [dma((2, steps))] * 2
         )
-        last[at, step].start()
-
-    for at, rows in enumerate(pieces):
-        for step in range(1, planes):
-            along[at, step].wait_recv()
-        whole = plane_in[0, rows]
-        for plane in range(1, planes):
-            whole = whole + plane_in[plane, rows]
-        out[core, chip, rows] = whole
-        for step in range(1, chips):
-            back[at, step] = pltpu.make_async_remote_copy(
-                src_ref=out.at[core, chip, rows],
-                dst_ref=out.at[core, chip, rows],
-                send_sem=back_send.at[at, step],
-                recv_sem=back_recv.at[at, step],
-                device_id=(2 * chip_at(step) + core, sr),
-                device_id_type=MESH,
-            )
-            back[at, step].start()
-        pass_on(at, rows, 0)
-    for at, rows in enumerate(pieces):
-        for step in range(1, chips):
-            back[at, step].wait_recv()
-            pass_on(at, rows, step)
-    for copy in last.values():
-        copy.wait_recv()
-    for copies in (pairs, across, along, back, last):
-        for copy in copies.values():
-            copy.wait_send()
-
-
-def all_sum(part, planes):
-    _, chips, rows, width = part.shape
-    dma = pltpu.SemaphoreType.DMA
-    cuts = [rows * at // PIECES // 8 * 8 for at in range(PIECES)] + [rows]
-    pieces = [slice(start, stop) for start, stop in zip(cuts, cuts[1:])]
-    vmem = pl.BlockSpec(memory_space=pltpu.VMEM)
+
+    shapes = [(2, chips, lows, tall, width) for tall in (rows, share)]
     return pl.pallas_call(
-        functools.partial(reduce_kernel, chips, planes, pieces),
-        out_shape=jax.ShapeDtypeStruct(part.shape, jnp.float32),
-        in_specs=[vmem],
-        out_specs=vmem,
+        functools.partial(gather_kernel, blocks, planes),
+        out_shape=[jax.ShapeDtypeStruct(shape, jnp.float32) for shape in shapes],
+        in_specs=[hbm, hbm, vmem],
+        out_specs=[vmem, vmem],
         scratch_shapes=[
-            pltpu.VMEM((chips, rows, width), jnp.float32),
-            pltpu.VMEM((chips, rows, width), jnp.float32),
-            pltpu.VMEM((chips, rows, width), jnp.float32),
-            pltpu.VMEM((planes, rows, width), jnp.float32),
+            pltpu.VMEM((length, series), observations.dtype),
+            memory(series, width),
+            memory(*shapes[0]),
+            memory(*shapes[1]),
+            dma((pieces,)),
+            dma((chips,)),
         ]
-        + [dma((PIECES, chips))] * 4
-        + [dma((PIECES, planes))] * 2
-        + [dma((PIECES, chips))] * 4,
+        + stream(share)
+        + stream(rows),
         compiler_params=pltpu.CompilerParams(collective_id=0, has_side_effects=True),
-        name="all_sum",
-    )(part)
+        name="gather",
+    )(observations, loadings, noise_precision.reshape(series // width, width))
 
 
 def shift_rows(value, steps):
@@ -398,27 +443,25 @@
 
 
 def smooth_kernel(
-    total_in, transition, filter_cov, gain, cov, observations, own, updated, moved,
+    total_in, info_in, transition, filter_cov, gain, cov, observations, own, updated, moved,
     drive, held, arrived,
 ):
     length = observations.shape[0]
     panel = pltpu.make_async_copy(observations, held, arrived)
     panel.start()
     width = transition.shape[0]
-    _, chips, rows, _ = total_in.shape
-    block = length // (2 * chips)
+    _, chips, lows, rows, _ = total_in.shape
     count = length // SLABS
     levels = (count - 1).bit_length()
-    info = jnp.concatenate(
-        [total_in[core, chip, block:, :] for chip in range(chips) for core in range(2)], axis=0
-    )
+    places = [
+        (core, chip, low) for chip in range(chips) for core in range(2) for low in range(lows)
+    ]
+    info = jnp.concatenate([info_in[place] for place in places], axis=0)
     closed = transition[...] - dot_high(filter_cov[...], dot_high(info, transition[...]))
     low, high = powers(closed.T, levels)
     cov_t = weights(filter_cov[...].T)
-    for chip in range(chips):
-        for core in range(2):
-            start = (2 * chip + core) * block
-            drive[start : start + block, :] = times(total_in[core, chip, :block, :], cov_t)
+    for at, place in enumerate(places):
+        drive[at * rows : (at + 1) * rows, :] = times(total_in[place], cov_t)
     slabs = [drive[pl.ds(at, count, stride=SLABS), :] for at in range(SLABS)]
     filtered = scan_slabs(slabs, low, high, False)
     coupled = weights(dot_high(gain[...], transition[...]).T)
@@ -429,6 +472,7 @@
     smooth = scan_slabs(back, low, high, True)
     for at in range(SLABS):
         drive[pl.ds(at, count, stride=SLABS), :] = smooth[at]
+    block = own.shape[0]
     place = pl.multiple_of(lax.axis_index("tm") * block, block)
     own[...] = drive[pl.ds(place, block), :]
     whole = drive[...]
@@ -473,8 +517,7 @@
     width = transition.shape[0]
     length = observations.shape[0]
     steps_dev = length // blocks
-    part = project(observations, loadings, noise_precision, blocks)
-    summed = all_sum(part, planes)
+    summed = gather(observations, loadings, noise_precision, blocks, planes)
     vmem = pl.BlockSpec(memory_space=pltpu.VMEM)
     series = observations.shape[1]
     return pl.pallas_call(
@@ -484,7 +527,7 @@
             jax.ShapeDtypeStruct((series, width), jnp.float32),
             jax.ShapeDtypeStruct((width, width), jnp.float32),
         ],
-        in_specs=[vmem] * 5 + [pl.BlockSpec(memory_space=pl.ANY)],
+        in_specs=[vmem] * 6 + [pl.BlockSpec(memory_space=pl.ANY)],
         out_specs=[vmem] * 3,
         scratch_shapes=[
             pltpu.VMEM((length, width), jnp.float32),
@@ -492,7 +535,7 @@
             pltpu.SemaphoreType.DMA,
         ],
         name="smooth",
-    )(summed, transition, filter_cov, smoother_gain, smoothed_cov, observations)
+    )(*summed, transition, filter_cov, smoother_gain, smoothed_cov, observations)
 
 
 def solution(mesh):

time: 48.4 us -> 42.8 us (0.88)
  Pallas kernels: 47.5 us -> 41.9 us
    pallas_call x2 -> x1, Pallas kernels: 30.7 us -> 24.9 us  [gather(): pl.pallas_call(functools.partial(gather_kernel, blocks, planes), out_shap...]
where the time goes in v2:
time: 42.8 us; the launch traced here: 42.6 us
  Pallas kernels  41.9 us (98%)
  between operations  0.64 us (1%)
    pallas_call x1, Pallas kernels, gather(): pl.pallas_call(functools.partial(gather_kernel, blocks, planes), out_shap...  24.9 us
    pallas_call x1, Pallas kernels, local(): pl.pallas_call(smooth_kernel, out_shape=[jax.ShapeDtypeStruct((steps_dev,...  17 us

profile of v2, /device:TPU:0, one launch (start us, length us, event | category | flops | bytes accessed | tf_op | source)
XLA Modules:
  0.0 42.6 jit_solution(2606325276858097169)
XLA Ops:
  0.6 24.9 %gather.1 = (f32[2,4,2,64,128]{4,3,2,1,0:T(8,128)}, f32[2,4,2,8,128]{4,3,2,1,0:T(8,128)}) custom-call(bf16[1024,2048]{1,0:T(8,128)(2,1)} %observations.3, f32[2048,128]{1,0:T(8,128)} %loadings.1, f32[16,128]{1,0:T(8,128)} %bitcast.1), custom_call_target="tpu_custom_call" | custom-call | tf_op jit(solution)/shard_map/gather/pallas_call | solution.py:263
  25.6 17.0 %smooth.1 = (f32[128,128]{1,0:T(8,128)}, f32[2048,128]{1,0:T(8,128)}, f32[128,128]{1,0:T(8,128)}) custom-call(f32[2,4,2,64,128]{4,3,2,1,0:T(8,128)} %get-tuple-element.5.total_in, f32[2,4,2,8,128]{4,3,2,1,0:T(8,128)} %get-tuple-element.6.info_in, f32[128,128]{1,0:T(8,128)} %transition.1, f32[128,128]{1,0:T(8,128)} %filter_cov.1, f32[128,128]{1,0:T(8,128)} %gain.1, ...), custom_call_target="tpu_custom_call" | custom-call | tf_op jit(solution)/shard_map/smooth/pallas_call | solution.py:523

commit v3 on v2

--- a/solution.py
+++ b/solution.py
@@ -44,8 +44,8 @@
 
 
 def gather_kernel(
-    blocks, planes, observations, loadings, precision, out, out_info,
-    panel, rows_in, part, part_info, *scratch,
+    blocks, planes, observations, loadings, precision, transition, filter_cov, gain, drive,
+    near, far, out, out_info, panel, rows_in, part, part_info, *scratch,
 ):
     chips = blocks // 2
     _, _, lows, rows, width = part.shape
@@ -223,21 +223,53 @@
     for step in waiting:
         large.to_cube(step)
     small.to_far()
+    for _ in powers(gain[...].T, near.at[1], far.at[1]):
+        pass
+    cov_t = weights(filter_cov[...].T)
+    coupled = weights(dot_high(gain[...], transition[...]).T)
     large.to_far()
     small.to_back()
     large.to_back()
-    for stream in (small, large):
-        for step in order[:-1]:
-            stream.to_last(step)
-    for stream in (small, large):
-        for step in order:
-            stream.wait(("last", step))
+    for step in order[:-1]:
+        small.to_last(step)
+    for step in order:
+        small.wait(("last", step))
+    places = [
+        (at, turn, half) for turn in range(chips) for at in range(2) for half in range(lows)
+    ]
+    info = jnp.concatenate([out_info[place] for place in places], axis=0)
+    closed = transition[...] - dot_high(filter_cov[...], dot_high(info, transition[...]))
+    for _ in powers(closed.T, near.at[0], far.at[0]):
+        pass
+
+    def enter(at, step):
+        source = lax.rem(chip + chips - step // lows, chips)
+        half = lax.rem(low + lows - step % lows, lows)
+        start = pl.multiple_of((2 * source + at) * block + half * rows, rows)
+        drive[pl.ds(start, rows), :] = times(out[at, source, half], cov_t)
+
+    enter(core, 0)
+    for step in order[:-1]:
+        large.to_last(step)
+        enter(core, step)
+    for step in [0] + order[:-1]:
+        large.wait(("last", step))
+        enter(other, step)
+    count = length // SLABS
+    slabs = [drive[pl.ds(at, count, stride=SLABS), :] for at in range(SLABS)]
+    filtered = scan_slabs(slabs, near.at[0], far.at[0], False)
+    final = lax.broadcasted_iota(jnp.int32, (count, width), 0) == count - 1
+    back = [each - times(each, coupled) for each in filtered]
+    back[-1] = jnp.where(final, filtered[-1], back[-1])
+    smooth = scan_slabs(back, near.at[1], far.at[1], True)
+    for at in range(SLABS):
+        drive[pl.ds(at, count, stride=SLABS), :] = smooth[at]
     for stream in (small, large):
         for copy in stream.sent:
             copy.wait_send()
 
 
-def gather(observations, loadings, noise_precision, blocks, planes):
+def gather(observations, loadings, noise_precision, transition, filter_cov, gain, blocks, planes):
     length, series = observations.shape
     width = loadings.shape[1]
     chips = blocks // 2
@@ -250,6 +282,7 @@
     vmem = pl.BlockSpec(memory_space=pltpu.VMEM)
     hbm = pl.BlockSpec(memory_space=pl.ANY)
     steps = chips * lows
+    levels = (length // SLABS - 1).bit_length()
 
     def memory(*shape):
         return pltpu.VMEM(shape, jnp.float32)
@@ -262,10 +295,14 @@
     shapes = [(2, chips, lows, tall, width) for tall in (rows, share)]
     return pl.pallas_call(
         functools.partial(gather_kernel, blocks, planes),
-        out_shape=[jax.ShapeDtypeStruct(shape, jnp.float32) for shape in shapes],
-        in_specs=[hbm, hbm, vmem],
-        out_specs=[vmem, vmem],
+        out_shape=jax.ShapeDtypeStruct((length, width), jnp.float32),
+        in_specs=[hbm, hbm] + [vmem] * 4,
+        out_specs=vmem,
         scratch_shapes=[
+            pltpu.VMEM((2, SLABS - 1, 2 * width, 2 * width), jnp.bfloat16),
+            pltpu.VMEM((2, levels, 2 * width, 2 * width), jnp.bfloat16),
+            memory(*shapes[0]),
+            memory(*shapes[1]),
             pltpu.VMEM((length, series), observations.dtype),
             memory(series, width),
             memory(*shapes[0]),
@@ -277,7 +314,10 @@
         + stream(rows),
         compiler_params=pltpu.CompilerParams(collective_id=0, has_side_effects=True),
         name="gather",
-    )(observations, loadings, noise_precision.reshape(series // width, width))
+    )(
+        observations, loadings, noise_precision.reshape(series // width, width),
+        transition, filter_cov, gain,
+    )
 
 
 def shift_rows(value, steps):
@@ -288,16 +328,22 @@
     return jnp.where(keep, moved, 0.0)
 
 
-def powers(matrix, count):
-    low = [matrix]
-    while len(low) < SLABS:
-        low = low + [dot_high(low[-1], each) for each in low]
-    high = []
-    square = low[-1]
-    for _ in range(count - 1):
+def powers(matrix, low, high):
+    made = [matrix]
+    low[0] = weights(matrix)
+    while len(made) < SLABS:
+        fresh = [dot_high(made[-1], each) for each in made]
+        for each in fresh:
+            if len(made) < SLABS - 1:
+                low[len(made)] = weights(each)
+            made.append(each)
+        yield
+    square = made[-1]
+    high[0] = weights(square)
+    for level in range(1, high.shape[0]):
         square = dot_high(square, square)
-        high.append(square)
-    return [weights(each) for each in low], [weights(low[-1])] + [weights(each) for each in high]
+        high[level] = weights(square)
+        yield
 
 
 def scan_slabs(slabs, low, high, reverse):
@@ -307,8 +353,8 @@
     for before, now in zip(order, order[1:]):
         part[now] = slabs[now] + times(part[before], low[0])
     ends = part[order[-1]]
-    for level, power in enumerate(high):
-        ends = ends + times(shift_rows(ends, sign * 2**level), power)
+    for level in range(high.shape[0]):
+        ends = ends + times(shift_rows(ends, sign * 2**level), high[level])
     carry = shift_rows(ends, sign)
     out = [None] * SLABS
     for place, now in enumerate(order[:-1]):
@@ -443,35 +489,11 @@
 
 
 def smooth_kernel(
-    total_in, info_in, transition, filter_cov, gain, cov, observations, own, updated, moved,
-    drive, held, arrived,
+    drive, gain, cov, observations, own, updated, moved, held, arrived,
 ):
-    length = observations.shape[0]
+    length, width = drive.shape
     panel = pltpu.make_async_copy(observations, held, arrived)
     panel.start()
-    width = transition.shape[0]
-    _, chips, lows, rows, _ = total_in.shape
-    count = length // SLABS
-    levels = (count - 1).bit_length()
-    places = [
-        (core, chip, low) for chip in range(chips) for core in range(2) for low in range(lows)
-    ]
-    info = jnp.concatenate([info_in[place] for place in places], axis=0)
-    closed = transition[...] - dot_high(filter_cov[...], dot_high(info, transition[...]))
-    low, high = powers(closed.T, levels)
-    cov_t = weights(filter_cov[...].T)
-    for at, place in enumerate(places):
-        drive[at * rows : (at + 1) * rows, :] = times(total_in[place], cov_t)
-    slabs = [drive[pl.ds(at, count, stride=SLABS), :] for at in range(SLABS)]
-    filtered = scan_slabs(slabs, low, high, False)
-    coupled = weights(dot_high(gain[...], transition[...]).T)
-    last = lax.broadcasted_iota(jnp.int32, (count, width), 0) == count - 1
-    back = [each - times(each, coupled) for each in filtered]
-    back[-1] = jnp.where(last, filtered[-1], back[-1])
-    low, high = powers(gain[...].T, levels)
-    smooth = scan_slabs(back, low, high, True)
-    for at in range(SLABS):
-        drive[pl.ds(at, count, stride=SLABS), :] = smooth[at]
     block = own.shape[0]
     place = pl.multiple_of(lax.axis_index("tm") * block, block)
     own[...] = drive[pl.ds(place, block), :]
@@ -489,7 +511,7 @@
     sums = sums[:width] + sums[width:]
     previous = sums[:, :width] + sums[:, width : 2 * width]
     lagged = sums[:, 2 * width : 3 * width] + sums[:, 3 * width :]
-    final = smooth[-1][count - 8 :, :]
+    final = whole[length - 8 :, :]
     final = jnp.where(lax.broadcasted_iota(jnp.int32, final.shape, 0) == 7, final, 0.0)
     total = previous + dot_first(final, final)
     total = total + length * cov[...]
@@ -517,7 +539,10 @@
     width = transition.shape[0]
     length = observations.shape[0]
     steps_dev = length // blocks
-    summed = gather(observations, loadings, noise_precision, blocks, planes)
+    factors = gather(
+        observations, loadings, noise_precision, transition, filter_cov, smoother_gain,
+        blocks, planes,
+    )
     vmem = pl.BlockSpec(memory_space=pltpu.VMEM)
     series = observations.shape[1]
     return pl.pallas_call(
@@ -527,15 +552,14 @@
             jax.ShapeDtypeStruct((series, width), jnp.float32),
             jax.ShapeDtypeStruct((width, width), jnp.float32),
         ],
-        in_specs=[vmem] * 6 + [pl.BlockSpec(memory_space=pl.ANY)],
+        in_specs=[vmem] * 3 + [pl.BlockSpec(memory_space=pl.ANY)],
         out_specs=[vmem] * 3,
         scratch_shapes=[
-            pltpu.VMEM((length, width), jnp.float32),
             pltpu.VMEM((length, series), observations.dtype),
             pltpu.SemaphoreType.DMA,
         ],
         name="smooth",
-    )(*summed, transition, filter_cov, smoother_gain, smoothed_cov, observations)
+    )(factors, smoother_gain, smoothed_cov, observations)
 
 
 def solution(mesh):

time: 42.8 us -> 41.1 us (0.960)
  Pallas kernels: 41.9 us -> 40.1 us
    pallas_call x1, Pallas kernels: 17 us -> 9.34 us  [local(): pl.pallas_call(smooth_kernel, out_shape=[jax.ShapeDtypeStruct((steps_dev,...]
    pallas_call x1, Pallas kernels: 24.9 us -> 30.8 us  [gather(): pl.pallas_call(functools.partial(gather_kernel, blocks, planes), out_shap...]
where the time goes in v3:
time: 41.1 us; the launch traced here: 40.8 us
  Pallas kernels  40.1 us (98%)
  between operations  0.64 us (2%)
    pallas_call x1, Pallas kernels, gather(): pl.pallas_call(functools.partial(gather_kernel, blocks, planes), out_shap...  30.8 us
    pallas_call x1, Pallas kernels, local(): pl.pallas_call(smooth_kernel, out_shape=[jax.ShapeDtypeStruct((steps_dev,...  9.34 us

profile of v3, /device:TPU:0, one launch (start us, length us, event | category | flops | bytes accessed | tf_op | source)
XLA Modules:
  0.0 40.8 jit_solution(4979488483311433819)
XLA Ops:
  0.6 30.8 %gather.1.drive = f32[1024,128]{1,0:T(8,128)} custom-call(bf16[1024,2048]{1,0:T(8,128)(2,1)} %observations.3, f32[2048,128]{1,0:T(8,128)} %loadings.1, f32[16,128]{1,0:T(8,128)} %bitcast.1, f32[128,128]{1,0:T(8,128)} %transition.1, f32[128,128]{1,0:T(8,128)} %filter_cov.1, f32[128,128]{1,0:T(8,128)} %gain.3), custom_call_target="tpu_custom_call" | custom-call | tf_op jit(solution)/shard_map/gather/pallas_call | solution.py:296
  31.4 9.3 %smooth.1 = (f32[128,128]{1,0:T(8,128)}, f32[2048,128]{1,0:T(8,128)}, f32[128,128]{1,0:T(8,128)}) custom-call(f32[1024,128]{1,0:T(8,128)} %gather.1.drive, f32[128,128]{1,0:T(8,128)} %gain.3, f32[128,128]{1,0:T(8,128)} %cov.1, bf16[1024,2048]{1,0:T(8,128)(2,1)} %observations.3), custom_call_target="tpu_custom_call" | custom-call | tf_op jit(solution)/shard_map/smooth/pallas_call | solution.py:548

commit v4 on v3

--- a/solution.py
+++ b/solution.py
@@ -10,6 +10,7 @@
 MESH = pl.DeviceIdType.MESH
 SLABS = 8
 PIVOTS = 4
+GRANT = 24 * 2**20
 
 
 def dot_high(left, right):
@@ -44,8 +45,9 @@
 
 
 def gather_kernel(
-    blocks, planes, observations, loadings, precision, transition, filter_cov, gain, drive,
-    near, far, out, out_info, panel, rows_in, part, part_info, *scratch,
+    blocks, planes, observations, loadings, precision_in, transition_in, filter_cov_in, gain_in,
+    drive, panel, precision, transition, filter_cov, gain, small_done,
+    near, far, out, out_info, rows_in, part, part_info, *scratch,
 ):
     chips = blocks // 2
     _, _, lows, rows, width = part.shape
@@ -77,6 +79,14 @@
         return (tm, lax.rem(high + step, highs) * lows + low)
 
     loads_done, panel_done = scratch[:2]
+    given = (precision_in, transition_in, filter_cov_in, gain_in)
+    kept = (precision, transition, filter_cov, gain)
+    smalls = [
+        pltpu.make_async_copy(source, target, small_done.at[at])
+        for at, (source, target) in enumerate(zip(given, kept))
+    ]
+    for copy in smalls:
+        copy.start()
     pieces = loads_done.shape[0]
     depth = series // pieces
     loads = []
@@ -106,6 +116,7 @@
 
     both = None
     weighted = []
+    smalls[0].wait()
     for at in range(pieces):
         here = slice(at * depth, (at + 1) * depth)
         columns = [
@@ -223,6 +234,8 @@
     for step in waiting:
         large.to_cube(step)
     small.to_far()
+    for copy in smalls[1:]:
+        copy.wait()
     for _ in powers(gain[...].T, near.at[1], far.at[1]):
         pass
     cov_t = weights(filter_cov[...].T)
@@ -269,6 +282,10 @@
             copy.wait_send()
 
 
+def stay(*arrays):
+    return [pltpu.with_memory_space_constraint(array, pltpu.HBM) for array in arrays]
+
+
 def gather(observations, loadings, noise_precision, transition, filter_cov, gain, blocks, planes):
     length, series = observations.shape
     width = loadings.shape[1]
@@ -280,7 +297,7 @@
     pieces = min(4, series // width)
     dma = pltpu.SemaphoreType.DMA
     vmem = pl.BlockSpec(memory_space=pltpu.VMEM)
-    hbm = pl.BlockSpec(memory_space=pl.ANY)
+    hbm = pl.BlockSpec(memory_space=pltpu.HBM)
     steps = chips * lows
     levels = (length // SLABS - 1).bit_length()
 
@@ -295,15 +312,22 @@
     shapes = [(2, chips, lows, tall, width) for tall in (rows, share)]
     return pl.pallas_call(
         functools.partial(gather_kernel, blocks, planes),
-        out_shape=jax.ShapeDtypeStruct((length, width), jnp.float32),
-        in_specs=[hbm, hbm] + [vmem] * 4,
-        out_specs=vmem,
+        out_shape=[
+            pltpu.VMEM((length, width), jnp.float32),
+            pltpu.VMEM((length, series), observations.dtype),
+        ],
+        in_specs=[hbm] * 6,
+        out_specs=[vmem, vmem],
         scratch_shapes=[
+            memory(series // width, width),
+            memory(width, width),
+            memory(width, width),
+            memory(width, width),
+            dma((4,)),
             pltpu.VMEM((2, SLABS - 1, 2 * width, 2 * width), jnp.bfloat16),
             pltpu.VMEM((2, levels, 2 * width, 2 * width), jnp.bfloat16),
             memory(*shapes[0]),
             memory(*shapes[1]),
-            pltpu.VMEM((length, series), observations.dtype),
             memory(series, width),
             memory(*shapes[0]),
             memory(*shapes[1]),
@@ -312,11 +336,15 @@
         ]
         + stream(share)
         + stream(rows),
-        compiler_params=pltpu.CompilerParams(collective_id=0, has_side_effects=True),
+        compiler_params=pltpu.CompilerParams(
+            collective_id=0, has_side_effects=True, vmem_limit_bytes=GRANT
+        ),
         name="gather",
     )(
-        observations, loadings, noise_precision.reshape(series // width, width),
-        transition, filter_cov, gain,
+        *stay(
+            observations, loadings, noise_precision.reshape(series // width, width),
+            transition, filter_cov, gain,
+        )
     )
 
 
@@ -489,14 +517,20 @@
 
 
 def smooth_kernel(
-    drive, gain, cov, observations, own, updated, moved, held, arrived,
+    drive, held, gain_in, cov_in, own, updated, moved_out, gain, cov, staged, moved,
+    small_done, own_done, moved_done, part_done,
 ):
     length, width = drive.shape
-    panel = pltpu.make_async_copy(observations, held, arrived)
-    panel.start()
+    smalls = [
+        pltpu.make_async_copy(gain_in, gain, small_done.at[0]),
+        pltpu.make_async_copy(cov_in, cov, small_done.at[1]),
+    ]
+    for copy in smalls:
+        copy.start()
     block = own.shape[0]
     place = pl.multiple_of(lax.axis_index("tm") * block, block)
-    own[...] = drive[pl.ds(place, block), :]
+    owned = pltpu.make_async_copy(drive.at[pl.ds(place, block), :], own, own_done)
+    owned.start()
     whole = drive[...]
     high, rest = halves(whole)
     factors = high.T
@@ -511,24 +545,33 @@
     sums = sums[:width] + sums[width:]
     previous = sums[:, :width] + sums[:, width : 2 * width]
     lagged = sums[:, 2 * width : 3 * width] + sums[:, 3 * width :]
+    for copy in smalls:
+        copy.wait()
     final = whole[length - 8 :, :]
     final = jnp.where(lax.broadcasted_iota(jnp.int32, final.shape, 0) == 7, final, 0.0)
     total = previous + dot_first(final, final)
     total = total + length * cov[...]
     previous = previous + (length - 1) * cov[...]
     lagged = lagged + (length - 1) * dot_high(cov[...], gain[...].T)
-    panel.wait()
-    series = updated.shape[0]
+    series = held.shape[1]
     parts = [slice(start, min(start + 256, series)) for start in range(0, series, 256)]
     for part in parts:
-        updated[part, :] = jnp.dot(
+        staged[part, :] = jnp.dot(
             factors, held[:, part], preferred_element_type=jnp.float32
         ).T
     total, previous = invert([total, previous])
     total = weights(total)
-    for part in parts:
-        updated[part, :] = times(updated[part, :], total)
     moved[...] = dot_high(lagged, previous)
+    writes = [owned, pltpu.make_async_copy(moved, moved_out, moved_done)]
+    writes[-1].start()
+    for at, part in enumerate(parts):
+        staged[part, :] = times(staged[part, :], total)
+        writes.append(
+            pltpu.make_async_copy(staged.at[part, :], updated.at[part, :], part_done.at[at])
+        )
+        writes[-1].start()
+    for copy in writes:
+        copy.wait()
 
 
 def local(
@@ -539,7 +582,7 @@
     width = transition.shape[0]
     length = observations.shape[0]
     steps_dev = length // blocks
-    factors = gather(
+    factors, panel = gather(
         observations, loadings, noise_precision, transition, filter_cov, smoother_gain,
         blocks, planes,
     )
@@ -552,14 +595,21 @@
             jax.ShapeDtypeStruct((series, width), jnp.float32),
             jax.ShapeDtypeStruct((width, width), jnp.float32),
         ],
-        in_specs=[vmem] * 3 + [pl.BlockSpec(memory_space=pl.ANY)],
-        out_specs=[vmem] * 3,
+        in_specs=[vmem] * 2 + [pl.BlockSpec(memory_space=pltpu.HBM)] * 2,
+        out_specs=[pl.BlockSpec(memory_space=pltpu.HBM)] * 3,
         scratch_shapes=[
-            pltpu.VMEM((length, series), observations.dtype),
+            pltpu.VMEM((width, width), jnp.float32),
+            pltpu.VMEM((width, width), jnp.float32),
+            pltpu.VMEM((series, width), jnp.float32),
+            pltpu.VMEM((width, width), jnp.float32),
+            pltpu.SemaphoreType.DMA((2,)),
             pltpu.SemaphoreType.DMA,
+            pltpu.SemaphoreType.DMA,
+            pltpu.SemaphoreType.DMA((pl.cdiv(series, 256),)),
         ],
+        compiler_params=pltpu.CompilerParams(vmem_limit_bytes=GRANT),
         name="smooth",
-    )(factors, smoother_gain, smoothed_cov, observations)
+    )(factors, panel, *stay(smoother_gain, smoothed_cov))
 
 
 def solution(mesh):

time: 41.1 us -> 37.5 us (0.912)
  Pallas kernels: 40.1 us -> 36.5 us
    pallas_call x1, Pallas kernels: 9.34 us -> 7.33 us  [local(): pl.pallas_call(smooth_kernel, out_shape=[jax.ShapeDtypeStruct((steps_dev,...]
    pallas_call x1, Pallas kernels: 30.8 us -> 29.2 us  [gather(): pl.pallas_call(functools.partial(gather_kernel, blocks, planes), out_shap...]
where the time goes in v4:
time: 37.5 us; the launch traced here: 37.2 us
  Pallas kernels  36.5 us (97%)
  between operations  0.64 us (2%)
    pallas_call x1, Pallas kernels, gather(): pl.pallas_call(functools.partial(gather_kernel, blocks, planes), out_shap...  29.2 us
    pallas_call x1, Pallas kernels, local(): pl.pallas_call(smooth_kernel, out_shape=[jax.ShapeDtypeStruct((steps_dev,...  7.33 us

profile of v4, /device:TPU:0, one launch (start us, length us, event | category | flops | bytes accessed | tf_op | source)
XLA Modules:
  0.0 37.2 jit_solution(13248907575799608193)
XLA Ops:
  0.6 29.2 %gather.1 = (f32[1024,128]{1,0:T(8,128)S(1)}, bf16[1024,2048]{1,0:T(8,128)(2,1)S(1)}) custom-call(bf16[1024,2048]{1,0:T(8,128)(2,1)} %observations.1, f32[2048,128]{1,0:T(8,128)} %loadings.1, f32[16,128]{1,0:T(8,128)} %bitcast.1, f32[128,128]{1,0:T(8,128)} %transition_in.1, f32[128,128]{1,0:T(8,128)} %filter_cov_in.1, f32[128,128]{1,0:T(8,128)} %gain_in.3), custom_call_target="tpu_custom_call" | custom-call | tf_op jit(solution)/shard_map/gather/pallas_call | solution.py:313
  29.8 7.3 %smooth.1 = (f32[128,128]{1,0:T(8,128)}, f32[2048,128]{1,0:T(8,128)}, f32[128,128]{1,0:T(8,128)}) custom-call(f32[1024,128]{1,0:T(8,128)S(1)} %get-tuple-element.5.drive, bf16[1024,2048]{1,0:T(8,128)(2,1)S(1)} %get-tuple-element.6.held, f32[128,128]{1,0:T(8,128)} %gain_in.3, f32[128,128]{1,0:T(8,128)} %cov_in.1), custom_call_target="tpu_custom_call" | custom-call | tf_op jit(solution)/shard_map/smooth/pallas_call | solution.py:591

commit v5 on v4

--- a/solution.py
+++ b/solution.py
@@ -47,7 +47,7 @@
 def gather_kernel(
     blocks, planes, observations, loadings, precision_in, transition_in, filter_cov_in, gain_in,
     drive, panel, precision, transition, filter_cov, gain, small_done,
-    near, far, out, out_info, rows_in, part, part_info, *scratch,
+    tables, out, out_info, rows_in, part, part_info, *scratch,
 ):
     chips = blocks // 2
     _, _, lows, rows, width = part.shape
@@ -64,10 +64,30 @@
     low = lax.rem(sr, lows)
     high = sr // lows
     partner = (2 * chip + other, sr)
-    order = list(range(lows, steps)) + list(range(lows))[::-1]
+    turns = sorted(range(1, chips), key=lambda turn: -turn.bit_count()) + [0]
+    order = [turn * lows + half for turn in turns for half in range(lows)[::-1]]
+    nearest = order[:-1][::-1]
+
+    def across_to(turn):
+        place = 0
+        for bit in range((chips - 1).bit_length()):
+            mine = lax.rem(chip // 2**bit + turn // 2**bit, 2)
+            place = place + mine * 2**bit
+        return place
+
+    def across_from(turn):
+        return across_to(turn)
+
+    if chips & (chips - 1):
+
+        def across_to(turn):
+            return lax.rem(chip + turn, chips)
+
+        def across_from(turn):
+            return lax.rem(chip + chips - turn, chips)
 
     def chip_at(step):
-        return lax.rem(chip + step // lows, chips)
+        return across_to(step // lows)
 
     def low_at(step):
         return lax.rem(low + step % lows, lows)
@@ -98,8 +118,8 @@
         loads[-1].start()
     tall = 2 * block
     panels = {}
-    for step in list(range(1, chips)) + [0]:
-        start = pl.multiple_of(lax.rem(chip + step, chips) * tall, tall)
+    for step in turns:
+        start = pl.multiple_of(across_to(step) * tall, tall)
         panels[step] = pltpu.make_async_copy(
             observations.at[pl.ds(start, tall), :],
             panel.at[pl.ds(start, tall), :],
@@ -178,7 +198,7 @@
 
         def to_far(self):
             total = self.mine[0]
-            for step in order[:-1]:
+            for step in nearest:
                 self.wait(("across", step))
                 total = total + self.cube_in[step]
             self.far_in[high] = total
@@ -202,7 +222,7 @@
 
         def to_last(self, step):
             self.wait(("back", step))
-            source = lax.rem(chip + chips - step // lows, chips)
+            source = across_from(step // lows)
             here = self.out.at[core, source, lax.rem(low + lows - step % lows, lows)]
             self.send(("last", step), here, here, self.last, step, partner)
 
@@ -211,9 +231,9 @@
     for step in order:
         small.to_pair(step)
     waiting = []
-    for turn in list(range(1, chips)) + [0]:
+    for turn in turns:
         panels[turn].wait()
-        source = lax.rem(chip + turn, chips)
+        source = across_to(turn)
         start = pl.multiple_of(source * tall, tall)
         proj = jnp.dot(
             panel[pl.ds(start, tall), :], weighted, preferred_element_type=jnp.float32
@@ -225,7 +245,7 @@
         fresh = [step for step in order if step // lows == turn]
         for step in fresh:
             large.to_pair(step)
-        if turn == 1 % chips:
+        if turn == turns[0]:
             for step in order:
                 small.to_cube(step)
         for step in waiting:
@@ -234,47 +254,48 @@
     for step in waiting:
         large.to_cube(step)
     small.to_far()
+    count = length // SLABS
     for copy in smalls[1:]:
         copy.wait()
-    for _ in powers(gain[...].T, near.at[1], far.at[1]):
-        pass
+    powers(gain[...].T, tables.at[1], count)
     cov_t = weights(filter_cov[...].T)
     coupled = weights(dot_high(gain[...], transition[...]).T)
     large.to_far()
     small.to_back()
     large.to_back()
-    for step in order[:-1]:
+    for step in nearest:
         small.to_last(step)
-    for step in order:
+    for step in [0] + nearest:
         small.wait(("last", step))
     places = [
         (at, turn, half) for turn in range(chips) for at in range(2) for half in range(lows)
     ]
     info = jnp.concatenate([out_info[place] for place in places], axis=0)
     closed = transition[...] - dot_high(filter_cov[...], dot_high(info, transition[...]))
-    for _ in powers(closed.T, near.at[0], far.at[0]):
-        pass
-
-    def enter(at, step):
-        source = lax.rem(chip + chips - step // lows, chips)
-        half = lax.rem(low + lows - step % lows, lows)
-        start = pl.multiple_of((2 * source + at) * block + half * rows, rows)
-        drive[pl.ds(start, rows), :] = times(out[at, source, half], cov_t)
-
-    enter(core, 0)
-    for step in order[:-1]:
+    powers(closed.T, tables.at[0], count)
+    for step in nearest:
         large.to_last(step)
-        enter(core, step)
-    for step in [0] + order[:-1]:
+
+    def enter(at):
+        tall = chips * lows * rows
+        given = out[at].reshape(tall, width)
+        entered = times(given, cov_t)
+        for turn in range(chips):
+            for half in range(lows):
+                start = pl.multiple_of((2 * turn + at) * block + half * rows, rows)
+                now = (turn * lows + half) * rows
+                drive[pl.ds(start, rows), :] = entered[now : now + rows]
+
+    enter(core)
+    for step in [0] + nearest:
         large.wait(("last", step))
-        enter(other, step)
-    count = length // SLABS
+    enter(other)
     slabs = [drive[pl.ds(at, count, stride=SLABS), :] for at in range(SLABS)]
-    filtered = scan_slabs(slabs, near.at[0], far.at[0], False)
+    filtered = scan_slabs(slabs, tables.at[0], False)
     final = lax.broadcasted_iota(jnp.int32, (count, width), 0) == count - 1
     back = [each - times(each, coupled) for each in filtered]
     back[-1] = jnp.where(final, filtered[-1], back[-1])
-    smooth = scan_slabs(back, near.at[1], far.at[1], True)
+    smooth = scan_slabs(back, tables.at[1], True)
     for at in range(SLABS):
         drive[pl.ds(at, count, stride=SLABS), :] = smooth[at]
     for stream in (small, large):
@@ -299,7 +320,7 @@
     vmem = pl.BlockSpec(memory_space=pltpu.VMEM)
     hbm = pl.BlockSpec(memory_space=pltpu.HBM)
     steps = chips * lows
-    levels = (length // SLABS - 1).bit_length()
+    entries = sum(radix - 1 for radix in [SLABS] + radices(length // SLABS))
 
     def memory(*shape):
         return pltpu.VMEM(shape, jnp.float32)
@@ -324,8 +345,7 @@
             memory(width, width),
             memory(width, width),
             dma((4,)),
-            pltpu.VMEM((2, SLABS - 1, 2 * width, 2 * width), jnp.bfloat16),
-            pltpu.VMEM((2, levels, 2 * width, 2 * width), jnp.bfloat16),
+            pltpu.VMEM((2, entries, 2 * width, 2 * width), jnp.bfloat16),
             memory(*shapes[0]),
             memory(*shapes[1]),
             memory(series, width),
@@ -356,37 +376,60 @@
     return jnp.where(keep, moved, 0.0)
 
 
-def powers(matrix, low, high):
-    made = [matrix]
-    low[0] = weights(matrix)
-    while len(made) < SLABS:
-        fresh = [dot_high(made[-1], each) for each in made]
-        for each in fresh:
-            if len(made) < SLABS - 1:
-                low[len(made)] = weights(each)
-            made.append(each)
-        yield
-    square = made[-1]
-    high[0] = weights(square)
-    for level in range(1, high.shape[0]):
-        square = dot_high(square, square)
-        high[level] = weights(square)
-        yield
-
-
-def scan_slabs(slabs, low, high, reverse):
+def radices(count):
+    bits = (count - 1).bit_length()
+    parts = -(-bits // 3)
+    return [2 ** (bits * (at + 1) // parts - bits * at // parts) for at in range(parts)][::-1]
+
+
+def powers(matrix, table, count):
+    levels = [SLABS] + radices(count)
+    base, start = matrix, 0
+    for at, radix in enumerate(levels):
+        made = [base]
+        top = radix if at + 1 < len(levels) else radix - 1
+        table[start] = weights(base)
+        while len(made) < top:
+            fresh = [dot_high(made[-1], each) for each in made][: top - len(made)]
+            for each in fresh:
+                if len(made) < radix - 1:
+                    table[start + len(made)] = weights(each)
+                made.append(each)
+        base = made[-1]
+        start += radix - 1
+
+
+def times_many(values, table, start):
+    width = values[0].shape[1]
+    left = jnp.concatenate([part for value in values for part in halves(value)], axis=1)
+    right = table[start : start + len(values)].reshape(2 * width * len(values), 2 * width)
+    out = jnp.dot(left, right, preferred_element_type=jnp.float32)
+    return out[:, :width] + out[:, width:]
+
+
+def scan_slabs(slabs, table, reverse):
     order = list(range(SLABS))[::-1] if reverse else list(range(SLABS))
     sign = -1 if reverse else 1
-    part = {order[0]: slabs[order[0]]}
-    for before, now in zip(order, order[1:]):
-        part[now] = slabs[now] + times(part[before], low[0])
-    ends = part[order[-1]]
-    for level in range(high.shape[0]):
-        ends = ends + times(shift_rows(ends, sign * 2**level), high[level])
+    part = [slabs[now] for now in order]
+    ends = part.pop()
+    ends = ends + times_many(part[::-1], table, 0)
+    start, stride = SLABS - 1, 1
+    for radix in radices(ends.shape[0]):
+        moved = [shift_rows(ends, sign * stride * at) for at in range(1, radix)]
+        ends = ends + times_many(moved, table, start)
+        start += radix - 1
+        stride *= radix
+    size = 1
+    while size < SLABS:
+        for first in range(size, SLABS - 1, 2 * size):
+            for offset in range(min(size, SLABS - 1 - first)):
+                add = times(part[first - 1], table[offset])
+                part[first + offset] = part[first + offset] + add
+        size *= 2
     carry = shift_rows(ends, sign)
     out = [None] * SLABS
     for place, now in enumerate(order[:-1]):
-        out[now] = part[now] + times(carry, low[place])
+        out[now] = part[place] + times(carry, table[place])
     out[order[-1]] = ends
     return out
 

time: 37.5 us -> 35.4 us (0.944)
  Pallas kernels: 36.5 us -> 34.5 us
    pallas_call x1, Pallas kernels: 29.2 us -> 27.2 us  [gather(): pl.pallas_call(functools.partial(gather_kernel, blocks, planes), out_shap...]
where the time goes in v5:
time: 35.4 us; the launch traced here: 35.2 us
  Pallas kernels  34.5 us (97%)
  between operations  0.64 us (2%)
    pallas_call x1, Pallas kernels, gather(): pl.pallas_call(functools.partial(gather_kernel, blocks, planes), out_shap...  27.2 us
    pallas_call x1, Pallas kernels, local(): pl.pallas_call(smooth_kernel, out_shape=[jax.ShapeDtypeStruct((steps_dev,...  7.32 us

profile of v5, /device:TPU:0, one launch (start us, length us, event | category | flops | bytes accessed | tf_op | source)
XLA Modules:
  0.0 35.2 jit_solution(5193810144989587635)
XLA Ops:
  0.6 27.2 %gather.1 = (f32[1024,128]{1,0:T(8,128)S(1)}, bf16[1024,2048]{1,0:T(8,128)(2,1)S(1)}) custom-call(bf16[1024,2048]{1,0:T(8,128)(2,1)} %observations.1, f32[2048,128]{1,0:T(8,128)} %loadings.1, f32[16,128]{1,0:T(8,128)} %bitcast.1, f32[128,128]{1,0:T(8,128)} %transition_in.1, f32[128,128]{1,0:T(8,128)} %filter_cov_in.1, f32[128,128]{1,0:T(8,128)} %gain_in.3), custom_call_target="tpu_custom_call" | custom-call | tf_op jit(solution)/shard_map/gather/pallas_call | solution.py:334
  27.9 7.3 %smooth.1 = (f32[128,128]{1,0:T(8,128)}, f32[2048,128]{1,0:T(8,128)}, f32[128,128]{1,0:T(8,128)}) custom-call(f32[1024,128]{1,0:T(8,128)S(1)} %get-tuple-element.5.drive, bf16[1024,2048]{1,0:T(8,128)(2,1)S(1)} %get-tuple-element.6.held, f32[128,128]{1,0:T(8,128)} %gain_in.3, f32[128,128]{1,0:T(8,128)} %cov_in.1), custom_call_target="tpu_custom_call" | custom-call | tf_op jit(solution)/shard_map/smooth/pallas_call | solution.py:634

commit v6 on v5

--- a/solution.py
+++ b/solution.py
@@ -10,6 +10,7 @@
 MESH = pl.DeviceIdType.MESH
 SLABS = 8
 PIVOTS = 4
+LAG = 3
 GRANT = 24 * 2**20
 
 
@@ -94,6 +95,9 @@
 
     def member(step):
         return (2 * chip_at(step) + core, high * lows + low_at(step))
+
+    def mirror(step):
+        return (2 * chip_at(step) + other, high * lows + low_at(step))
 
     def level(step):
         return (tm, lax.rem(high + step, highs) * lows + low)
@@ -130,7 +134,8 @@
     barrier = pltpu.get_barrier_semaphore()
     pl.semaphore_signal(barrier, inc=1, device_id=partner, device_id_type=MESH)
     for step in range(1, steps):
-        pl.semaphore_signal(barrier, inc=1, device_id=member(step), device_id_type=MESH)
+        for device in (member(step), mirror(step)):
+            pl.semaphore_signal(barrier, inc=1, device_id=device, device_id_type=MESH)
     for step in range(1, highs):
         pl.semaphore_signal(barrier, inc=1, device_id=level(step), device_id_type=MESH)
 
@@ -145,22 +150,23 @@
         ]
         loads[at].wait()
         value = rows_in[here, :]
-        scaled = value * jnp.concatenate(columns, axis=0)
+        column = jnp.concatenate(columns, axis=0)
+        scaled = value * column
         pair = halves(scaled)
         weighted.append(pair[0])
-        left = jnp.concatenate(halves(value), axis=1)
-        right = jnp.concatenate(pair, axis=1)
+        top = value.astype(jnp.bfloat16)
+        rest = ((value - top.astype(jnp.float32)) * column).astype(jnp.bfloat16)
         each = lax.dot_general(
-            left, right, (((0,), (0,)), ((), ())), preferred_element_type=jnp.float32
+            top, jnp.concatenate(pair + (rest,), axis=1), (((0,), (0,)), ((), ())),
+            preferred_element_type=jnp.float32,
         )
         both = each if both is None else both + each
     weighted = jnp.concatenate(weighted, axis=0)
-    both = both[:width] + both[width:]
-    info = both[:, :width] + both[:, width:]
+    info = both[:, :width] + both[:, width : 2 * width] + both[:, 2 * width :].T
     for place in range(2 * steps):
         now = slice(place * share, (place + 1) * share)
         part_info[place // lows % 2, place // (2 * lows), place % lows] = info[now]
-    pl.semaphore_wait(barrier, 1 + steps - 1 + highs - 1)
+    pl.semaphore_wait(barrier, 1 + 2 * (steps - 1) + highs - 1)
 
     class Stream:
         def __init__(self, part, out, pair_in, mine, cube_in, far_in, pair, across, far, back, last):
@@ -208,7 +214,7 @@
                     self.far, step, level(step),
                 )
 
-        def to_back(self):
+        def to_back(self, both_cores):
             for step in range(1, highs):
                 self.wait(("far", step))
             total = self.far_in[0]
@@ -218,6 +224,8 @@
             here[...] = total
             for step in order[:-1]:
                 self.send(("back", step), here, here, self.back, step, member(step))
+                if both_cores:
+                    self.send(("last", step), here, here, self.last, step, mirror(step))
             self.send(("last", 0), here, here, self.last, 0, partner)
 
         def to_last(self, step):
@@ -242,29 +250,30 @@
             for half in range(lows):
                 now = slice(at * block + half * rows, at * block + (half + 1) * rows)
                 part[at, source, half] = proj[now]
-        fresh = [step for step in order if step // lows == turn]
-        for step in fresh:
+        waiting.append([step for step in order if step // lows == turn])
+        for step in waiting[-1]:
             large.to_pair(step)
-        if turn == turns[0]:
+        if turn == turns[min(2, chips - 1)]:
             for step in order:
                 small.to_cube(step)
-        for step in waiting:
+        if len(waiting) > LAG:
+            for step in waiting.pop(0):
+                large.to_cube(step)
+    for fresh in waiting:
+        for step in fresh:
             large.to_cube(step)
-        waiting = fresh
-    for step in waiting:
-        large.to_cube(step)
-    small.to_far()
     count = length // SLABS
     for copy in smalls[1:]:
         copy.wait()
+    small.to_far()
+    large.to_far()
     powers(gain[...].T, tables.at[1], count)
     cov_t = weights(filter_cov[...].T)
     coupled = weights(dot_high(gain[...], transition[...]).T)
-    large.to_far()
-    small.to_back()
-    large.to_back()
+    small.to_back(True)
+    large.to_back(False)
     for step in nearest:
-        small.to_last(step)
+        small.wait(("back", step))
     for step in [0] + nearest:
         small.wait(("last", step))
     places = [
@@ -500,13 +509,15 @@
             if g == order[0] and following < half:
                 coming = [pick(value[g], lane, half, following + j) for j in range(PIVOTS)]
         if following < half:
-            cross = [[spread(columns[ahead][j], spot + i) for j in range(PIVOTS)] for i in range(PIVOTS)]
-            moved = [[sum(solved[i][j] * cross[b][j] for j in range(PIVOTS)) for b in range(PIVOTS)] for i in range(PIVOTS)]
-            block = [[None] * PIVOTS for _ in range(PIVOTS)]
-            for a in range(PIVOTS):
-                for b in range(a, PIVOTS):
-                    take = sum(cross[a][i] * moved[i][b] for i in range(PIVOTS))
-                    block[a][b] = block[b][a] = spread(coming[b], spot + a) - take
+            moved = [sum(solved[i][j] * columns[ahead][j] for j in range(PIVOTS)) for i in range(PIVOTS)]
+            later = []
+            for b in range(PIVOTS):
+                take = sum(columns[ahead][i] * spread(moved[i], spot + b) for i in range(PIVOTS))
+                later.append(coming[b] - take)
+            block = [
+                [spread(later[max(i, j)], spot + min(i, j)) for j in range(PIVOTS)]
+                for i in range(PIVOTS)
+            ]
         here = (inner >= k) & (inner < k + PIVOTS)
         rows = []
         for i in range(PIVOTS):
@@ -524,7 +535,7 @@
     return jnp.concatenate(value, axis=0)
 
 
-def invert(matrices):
+def invert(matrices, between):
     size = matrices[0].shape[0]
     half = size // 2
     row_at = lax.broadcasted_iota(jnp.int32, (size, size), 0)
@@ -548,6 +559,7 @@
         over = jnp.concatenate([over, nothing], axis=0)
         upper.append(over)
         rest.append(m[half:] - dot_high(jnp.where(low, m[half:], 0.0), over))
+    between()
     packed = sweep(jnp.where(low, pltpu.roll(rest[1], half, 1), rest[0]))
     final = [jnp.where(low, 0.0, packed), jnp.where(low, 0.0, pltpu.roll(packed, half, 1))]
     out = []
@@ -560,7 +572,7 @@
 
 
 def smooth_kernel(
-    drive, held, gain_in, cov_in, own, updated, moved_out, gain, cov, staged, moved,
+    drive, held, gain_in, cov_in, own, updated, moved_out, gain, cov, staged, split, moved,
     small_done, own_done, moved_done, part_done,
 ):
     length, width = drive.shape
@@ -598,17 +610,20 @@
     lagged = lagged + (length - 1) * dot_high(cov[...], gain[...].T)
     series = held.shape[1]
     parts = [slice(start, min(start + 256, series)) for start in range(0, series, 256)]
-    for part in parts:
-        staged[part, :] = jnp.dot(
-            factors, held[:, part], preferred_element_type=jnp.float32
-        ).T
-    total, previous = invert([total, previous])
+
+    def fill():
+        for part in parts:
+            cross = jnp.dot(factors, held[:, part], preferred_element_type=jnp.float32).T
+            split[part, :] = jnp.concatenate(halves(cross), axis=1)
+
+    total, previous = invert([total, previous], fill)
     total = weights(total)
     moved[...] = dot_high(lagged, previous)
     writes = [owned, pltpu.make_async_copy(moved, moved_out, moved_done)]
     writes[-1].start()
     for at, part in enumerate(parts):
-        staged[part, :] = times(staged[part, :], total)
+        solved = jnp.dot(split[part, :], total, preferred_element_type=jnp.float32)
+        staged[part, :] = solved[:, :width] + solved[:, width:]
         writes.append(
             pltpu.make_async_copy(staged.at[part, :], updated.at[part, :], part_done.at[at])
         )
@@ -644,6 +659,7 @@
             pltpu.VMEM((width, width), jnp.float32),
             pltpu.VMEM((width, width), jnp.float32),
             pltpu.VMEM((series, width), jnp.float32),
+            pltpu.VMEM((series, 2 * width), jnp.bfloat16),
             pltpu.VMEM((width, width), jnp.float32),
             pltpu.SemaphoreType.DMA((2,)),
             pltpu.SemaphoreType.DMA,

time: 35.4 us -> 34.9 us (0.986)
  Pallas kernels: 34.5 us -> 34 us
    pallas_call x1, Pallas kernels: 27.2 us -> 26.8 us  [gather(): pl.pallas_call(functools.partial(gather_kernel, blocks, planes), out_shap...]
where the time goes in v6:
time: 34.9 us; the launch traced here: 34.7 us
  Pallas kernels  34 us (97%)
  between operations  0.64 us (2%)
    pallas_call x1, Pallas kernels, gather(): pl.pallas_call(functools.partial(gather_kernel, blocks, planes), out_shap...  26.8 us
    pallas_call x1, Pallas kernels, local(): pl.pallas_call(smooth_kernel, out_shape=[jax.ShapeDtypeStruct((steps_dev,...  7.22 us

profile of v6, /device:TPU:0, one launch (start us, length us, event | category | flops | bytes accessed | tf_op | source)
XLA Modules:
  0.0 34.7 jit_solution(15321167609152817469)
XLA Ops:
  0.6 26.8 %gather.1 = (f32[1024,128]{1,0:T(8,128)S(1)}, bf16[1024,2048]{1,0:T(8,128)(2,1)S(1)}) custom-call(bf16[1024,2048]{1,0:T(8,128)(2,1)} %observations.1, f32[2048,128]{1,0:T(8,128)} %loadings.1, f32[16,128]{1,0:T(8,128)} %bitcast.1, f32[128,128]{1,0:T(8,128)} %transition_in.1, f32[128,128]{1,0:T(8,128)} %filter_cov_in.1, f32[128,128]{1,0:T(8,128)} %gain_in.3), custom_call_target="tpu_custom_call" | custom-call | tf_op jit(solution)/shard_map/gather/pallas_call | solution.py:343
  27.4 7.2 %smooth.1 = (f32[128,128]{1,0:T(8,128)}, f32[2048,128]{1,0:T(8,128)}, f32[128,128]{1,0:T(8,128)}) custom-call(f32[1024,128]{1,0:T(8,128)S(1)} %get-tuple-element.5.drive, bf16[1024,2048]{1,0:T(8,128)(2,1)S(1)} %get-tuple-element.6.held, f32[128,128]{1,0:T(8,128)} %gain_in.3, f32[128,128]{1,0:T(8,128)} %cov_in.1), custom_call_target="tpu_custom_call" | custom-call | tf_op jit(solution)/shard_map/smooth/pallas_call | solution.py:649
